TPU v7x, 32 devices: a whole 2x2x4 slice. The times are simulated.
32 devices in a mesh: slab: 8 (over z, y), plane: 4 (over x, core).
Axes of the slice: x: 2, y: 2, z: 4, core: 2. Of those that a mesh axis runs over, the one named last changes fastest.
Arguments:
- tissue_v: float32 [32, 64, 128], P('slab', 'plane'), may hold values from -4 to 4
- tissue_gates: float32 [40, 32, 64, 128], P(None, 'slab', 'plane'), may hold values from 0 to 1
- tissue_diff: float32 [32, 64, 128], P('slab', 'plane'), may hold values from 0.2 to 1
- fibre_v: float32 [128, 2048], P('slab', 'plane'), may hold values from -4 to 4
- fibre_gates: float32 [40, 128, 2048], P(None, 'slab', 'plane'), may hold values from 0 to 1
- fibre_diff: float32 [128, 2048], P('slab', 'plane'), may hold values from 0.2 to 1
- gate_half: float32 [40], replicated, may hold values from -3 to 3
- gate_rate: float32 [40], replicated, may hold values from 0.5 to 20
- gate_cond: float32 [40], replicated, may hold values from 0.01 to 0.15
- gate_rev: float32 [40], replicated, may hold values from -2 to 2
- junc_cond: float32 [8], replicated, may hold values from 0.25 to 2
- junc_fibre: int32 [131072], P(('slab', 'plane')), may hold values from 0 to 15
- junc_fcell: int32 [131072], P(('slab', 'plane')), may hold values from 0 to 511
- junc_owner: int32 [131072, 1], P(('slab', 'plane')), may hold values from 0 to 31; in each aligned block of 4096 rows (0 to 4095, 4096 to 8191, ...) at most 256 rows name the same one
- junc_tcell: int32 [131072], P(('slab', 'plane')), may hold values from 0 to 8191
- junc_class: int32 [131072], P(('slab', 'plane')), may hold values from 0 to 7
Outputs:
- tissue_out: float32 [32, 64, 128], P('slab', 'plane')
- fibre_out: float32 [128, 2048], P('slab', 'plane')
Inputs may be any that keep to these rules, and one draw needn't show every extreme that they name: `junc_owner`: among the junctions held by one device, no tissue block is named by more than 256 of them, and some block is named by exactly 256. `junc_fibre`: A fibre of the slab group of the device that holds the junction. `junc_fcell`: A cell of the holding device's share of that fibre. `junc_tcell`: numbered over the owner's block in the order z, y, x with x fastest.
All inputs are finite; a program needn't handle non-finite values.
Results may differ from a plain program's by a relative error of at most 0.00005.
Values sent between devices are 32-bit elements; how exact they have to be, the bound alone decides.
A program may use at most 64 MiB of HBM per device.

v0:
```python
import jax
import jax.numpy as jnp
from jax import lax
from jax.sharding import PartitionSpec as P

STEPS = 14
time_step = 0.1
gate_slope = 2.0


def shift_pair(up, down, axis):
    count = lax.axis_size(axis)
    forward = [(i, i + 1) for i in range(count - 1)]
    backward = [(target, source) for source, target in forward]
    return (lax.ppermute(up, axis, forward), lax.ppermute(down, axis, backward))


def membrane(voltage, gates, gate_half, gate_rate, gate_cond, gate_rev):
    gate_shape = (gates.shape[0],) + (1,) * (gates.ndim - 1)
    gate_signs = (
        jnp.where(jnp.arange(gates.shape[0], dtype=jnp.int32) % 2 == 0, 1.0, -1.0)
        .astype(jnp.float32)
        .reshape(gate_shape)
    )
    shifted = voltage[None] - gate_half.reshape(gate_shape)
    steady = jax.nn.sigmoid(gate_signs * gate_slope * shifted)
    decay_factor = jnp.exp(
        -time_step * gate_rate.reshape(gate_shape) * (1.0 + jax.nn.sigmoid(shifted))
    )
    renewed = steady + (gates - steady) * decay_factor
    driving = gate_cond.reshape(gate_shape) * (voltage[None] - gate_rev.reshape(gate_shape))
    return (renewed, jnp.sum(driving * renewed, axis=0))


def line_count(length, offset, total):
    places = offset + jnp.arange(length, dtype=jnp.int32)
    return (places > 0).astype(jnp.float32) + (places < total - 1).astype(jnp.float32)


def class_gain(classes, junc_cond):
    return jnp.sum(
        jnp.where(
            classes[:, None] == jnp.arange(junc_cond.shape[0], dtype=jnp.int32)[None, :],
            junc_cond[None, :],
            jnp.zeros((), jnp.float32),
        ),
        axis=1,
    )


def make_onehot(indices, count):
    return (indices[:, None] == jnp.arange(count, dtype=jnp.int32)[None, :]).astype(jnp.float32)


def split_two(values):
    high = lax.reduce_precision(values, 8, 7)
    low = lax.reduce_precision(values - high, 8, 7)
    return (high, low)


def pick_split(rows, cols, table):
    depth, width = table.shape
    high, low = split_two(table)
    stacked = jnp.concatenate([high, low], axis=0).astype(jnp.bfloat16)
    onehot = rows[:, None] == (jnp.arange(2 * depth, dtype=jnp.int32) % depth)[None, :]
    rows_read = jnp.dot(onehot.astype(jnp.bfloat16), stacked, preferred_element_type=jnp.float32)
    chosen = cols[:, None] == jnp.arange(width, dtype=jnp.int32)[None, :]
    return jnp.sum(jnp.where(chosen, rows_read, 0.0), axis=1)


def place_split(rows, cols, values, depth, width):
    high, low = split_two(values)
    lanes = jnp.arange(2 * width, dtype=jnp.int32)
    both = jnp.where((lanes < width)[None, :], high[:, None], low[:, None])
    weighted = jnp.where(cols[:, None] == (lanes % width)[None, :], both, 0.0)
    onehot = (rows[:, None] == jnp.arange(depth, dtype=jnp.int32)[None, :]).astype(jnp.bfloat16)
    halves = lax.dot_general(
        onehot,
        weighted.astype(jnp.bfloat16),
        (((0,), (0,)), ((), ())),
        preferred_element_type=jnp.float32,
    )
    return halves[:, :width] + halves[:, width:]


def running_rank(owner_onehot):
    total, kinds = owner_onehot.shape
    tall = 128
    blocks = owner_onehot.astype(jnp.bfloat16).reshape(total // tall, tall, kinds)
    lower = jnp.tril(jnp.ones((tall, tall), jnp.bfloat16))
    within = jnp.einsum("ij,bjo->bio", lower, blocks, preferred_element_type=jnp.float32)
    sums = within[:, -1, :]
    count = total // tall
    before = jnp.tril(jnp.ones((count, count), jnp.float32), -1)
    ahead = jnp.dot(before, sums, precision=lax.Precision.HIGHEST)
    ranks = jnp.sum((within + ahead[:, None, :]).reshape(total, kinds) * owner_onehot, axis=1)
    return jnp.round(ranks).astype(jnp.int32) - 1


def place_values(row_onehot, col_onehot, values):
    weighted = col_onehot * values[:, None]
    return lax.dot_general(
        row_onehot,
        weighted,
        (((0,), (0,)), ((), ())),
        precision=lax.Precision.HIGHEST,
        preferred_element_type=jnp.float32,
    )


def trade_both(paired):
    return lax.all_to_all(paired, ("slab", "plane"), split_axis=1, concat_axis=1, tiled=True)


def body(
    tissue_v,
    tissue_gates,
    tissue_diff,
    fibre_v,
    fibre_gates,
    fibre_diff,
    gate_half,
    gate_rate,
    gate_cond,
    gate_rev,
    junc_cond,
    junc_fibre,
    junc_fcell,
    junc_owner,
    junc_tcell,
    junc_class,
):
    slab_count = lax.axis_size("slab")
    plane_count = lax.axis_size("plane")
    devices = slab_count * plane_count
    layers_dev, rows_dev, cols_dev = tissue_v.shape
    fibre_rows, fibre_cols = fibre_v.shape
    junctions = junc_fibre.shape[0]
    capacity = 2 * junctions // devices
    tissue_count = (
        line_count(layers_dev, lax.axis_index("slab") * layers_dev, layers_dev * slab_count)[
            :, None, None
        ]
        + line_count(rows_dev, lax.axis_index("plane") * rows_dev, rows_dev * plane_count)[
            None, :, None
        ]
        + line_count(cols_dev, 0, cols_dev)[None, None, :]
    )
    fibre_count = line_count(
        fibre_cols, lax.axis_index("plane") * fibre_cols, fibre_cols * plane_count
    )[None, :]
    fibre_cells = fibre_rows * fibre_cols
    fibre_width = 128
    fibre_grid_rows = fibre_cells // fibre_width
    tissue_grid_rows = layers_dev * rows_dev
    owners = junc_owner[:, 0]
    owner_onehot = make_onehot(owners, devices)
    rank_onehot = make_onehot(running_rank(owner_onehot), capacity)
    kinds = junc_cond.shape[0] + 1
    code = (junc_tcell * kinds + junc_class + 1).astype(jnp.float32)
    code_table = jnp.round(place_values(owner_onehot, rank_onehot, code)).astype(jnp.int32)
    fibre_index = (junc_fibre * fibre_cols + junc_fcell).astype(jnp.float32)
    fibre_table = jnp.round(place_values(owner_onehot, rank_onehot, fibre_index))
    own_cells = fibre_table.astype(jnp.int32).reshape(-1)
    sent_tables = jnp.stack([code_table // kinds, code_table % kinds - 1])
    got_tables = lax.all_to_all(
        sent_tables, ("slab", "plane"), split_axis=1, concat_axis=1, tiled=True
    )
    remote_cells = got_tables[0].reshape(-1)
    remote_gain = class_gain(got_tables[1].reshape(-1), junc_cond)
    own_gain = class_gain(sent_tables[1].reshape(-1), junc_cond)
    fibre_at_row, fibre_at_col = (own_cells // fibre_width, own_cells % fibre_width)
    cell_row, cell_col = (remote_cells // cols_dev, remote_cells % cols_dev)

    def advance(step_index, carry):
        tissue_now, tissue_state, fibre_now, fibre_state = carry
        fibre_grid = fibre_now.reshape(fibre_grid_rows, fibre_width)
        tissue_grid = tissue_now.reshape(tissue_grid_rows, cols_dev)
        end_pad = (0, cols_dev - fibre_rows)
        up = jnp.concatenate([tissue_now[:, -1], jnp.pad(fibre_now[:, -1], end_pad)[None]])
        down = jnp.concatenate([tissue_now[:, 0], jnp.pad(fibre_now[:, 0], end_pad)[None]])
        y_low, y_high = shift_pair(up, down, "plane")
        z_low, z_high = shift_pair(tissue_now[-1:], tissue_now[:1], "slab")
        fibre_at_slot = pick_split(fibre_at_row, fibre_at_col, fibre_grid)
        tissue_at_slot = pick_split(cell_row, cell_col, tissue_grid)
        paired = jnp.stack([fibre_at_slot, tissue_at_slot]).reshape(2, devices, capacity)
        traded = trade_both(paired).reshape(2, -1)
        current = remote_gain * (traded[0] - tissue_at_slot)
        fibre_current = own_gain * (fibre_at_slot - traded[1])
        tissue_source = place_split(
            cell_row, cell_col, current, tissue_grid_rows, cols_dev
        ).reshape(tissue_now.shape)
        fibre_source = place_split(
            fibre_at_row, fibre_at_col, fibre_current, fibre_grid_rows, fibre_width
        ).reshape(fibre_now.shape)
        sides = jnp.pad(tissue_now, ((0, 0), (0, 0), (1, 1)))
        neighbours = (
            jnp.concatenate([tissue_now[1:], z_high], axis=0)
            + jnp.concatenate([z_low, tissue_now[:-1]], axis=0)
            + jnp.concatenate([tissue_now[:, 1:], y_high[:-1, None]], axis=1)
            + jnp.concatenate([y_low[:-1, None], tissue_now[:, :-1]], axis=1)
            + sides[:, :, 2:]
            + sides[:, :, :-2]
        )
        tissue_lap = neighbours - tissue_count * tissue_now
        fibre_lap = (
            jnp.concatenate([fibre_now[:, 1:], y_high[-1, :fibre_rows, None]], axis=1)
            + jnp.concatenate([y_low[-1, :fibre_rows, None], fibre_now[:, :-1]], axis=1)
            - fibre_count * fibre_now
        )
        tissue_state, tissue_ionic = membrane(
            tissue_now, tissue_state, gate_half, gate_rate, gate_cond, gate_rev
        )
        fibre_state, fibre_ionic = membrane(
            fibre_now, fibre_state, gate_half, gate_rate, gate_cond, gate_rev
        )
        tissue_next = tissue_now + time_step * (
            tissue_diff * tissue_lap - tissue_ionic + tissue_source
        )
        fibre_next = fibre_now + time_step * (fibre_diff * fibre_lap - fibre_ionic - fibre_source)
        return (tissue_next, tissue_state, fibre_next, fibre_state)

    final = lax.fori_loop(0, STEPS, advance, (tissue_v, tissue_gates, fibre_v, fibre_gates))
    return (final[0], final[2])


def solution(mesh):
    in_specs = (
        P("slab", "plane", None),
        P(None, "slab", "plane", None),
        P("slab", "plane", None),
        P("slab", "plane"),
        P(None, "slab", "plane"),
        P("slab", "plane"),
        P(),
        P(),
        P(),
        P(),
        P(),
        P(("slab", "plane")),
        P(("slab", "plane")),
        P(("slab", "plane"), None),
        P(("slab", "plane")),
        P(("slab", "plane")),
    )
    out_specs = (P("slab", "plane", None), P("slab", "plane"))
    return jax.shard_map(body, mesh=mesh, in_specs=in_specs, out_specs=out_specs, check_vma=False)
```

profile of v0, /device:TPU:0, one launch (start us, length us, event | category | flops | bytes accessed | tf_op | source)
XLA Modules:
  0.0 494.1 jit_solution(6374147802733579538)
XLA Ops:
  5.3 7.3 %all-to-all-start.1 = ((s32[2,32,256]{2,0,1:T(2,128)}), s32[2,32,256]{2,0,1:T(2,128)S(1)}, u32[]{:S(2)}, u32[]{:S(2)}) async-start(s32[2,32,256]{2,0,1:T(2,128)} %copy.60), calls=%async_computation.1 | async-start | bytes 131072 | tf_op jit(solution)/shard_map/all_to_all | solution.py:166
  14.7 5.3 %all-to-all-done.1 = s32[2,32,256]{2,0,1:T(2,128)S(1)} async-done(((s32[2,32,256]{2,0,1:T(2,128)}), s32[2,32,256]{2,0,1:T(2,128)S(1)}, u32[]{:S(2)}, u32[]{:S(2)}) %all-to-all-start.1) | async-done | bytes 65568 | tf_op jit(solution)/shard_map/all_to_all | solution.py:166
  20.5 472.9 %while.20 = (s32[]{:T(128)}, f32[4,16,128]{2,1,0:T(8,128)S(1)}, f32[40,4,16,128]{3,2,1,0:T(8,128)S(1)}, f32[16,512]{1,0:T(8,128)S(1)}, f32[40,16,512]{2,1,0:T(8,...) while((s32[]{:T(128)}, f32[4,16,128]{2,1,0:T(8,128)S(1)}, ...), condition=%wide.region_8.9_spmd.clone, body=%wide.region_3.8_spmd.clone.sunk | while | flops 1107442944 | bytes 8335497 | solution.py:223
  22.0 4.5 collective-permute-start.1
  34.9 4.9 all-to-all-start
  42.5 4.6 all-to-all-done
  47.2 3.4 fusion.179
  50.7 3.4 fusion.173
  55.8 4.5 collective-permute-start.1
  68.6 4.9 all-to-all-start
  76.3 4.6 all-to-all-done
  84.5 3.4 fusion.173
  89.5 4.5 collective-permute-start.1
  102.4 4.9 all-to-all-start
  110.0 4.6 all-to-all-done
  114.8 3.4 fusion.179
  118.3 3.4 fusion.173
  123.3 4.5 collective-permute-start.1
  136.2 4.9 all-to-all-start
  143.8 4.6 all-to-all-done
  148.5 3.4 fusion.179
  152.0 3.4 fusion.173
  157.1 4.5 collective-permute-start.1
  169.9 4.9 all-to-all-start
  177.6 4.6 all-to-all-done
  182.3 3.4 fusion.179
  185.8 3.4 fusion.173
  190.8 4.5 collective-permute-start.1
  203.7 4.9 all-to-all-start
  211.3 4.6 all-to-all-done
  216.1 3.4 fusion.179
  219.6 3.4 fusion.173
  224.6 4.5 collective-permute-start.1
  237.5 4.9 all-to-all-start
  245.1 4.6 all-to-all-done
  249.8 3.4 fusion.179
  253.3 3.4 fusion.173
  258.4 4.5 collective-permute-start.1
  271.2 4.9 all-to-all-start
  278.9 4.6 all-to-all-done
  283.6 3.4 fusion.179
  287.1 3.4 fusion.173
  292.1 4.5 collective-permute-start.1
  305.0 4.9 all-to-all-start
  312.6 4.6 all-to-all-done
  317.4 3.4 fusion.179
  320.9 3.4 fusion.173
  325.9 4.5 collective-permute-start.1
  338.8 4.9 all-to-all-start
  346.4 4.6 all-to-all-done
  351.1 3.4 fusion.179
  359.7 4.5 collective-permute-start.1
  372.5 4.9 all-to-all-start
  380.2 4.6 all-to-all-done
  384.9 3.4 fusion.179
  393.4 4.5 collective-permute-start.1
  406.3 4.9 all-to-all-start
  413.9 4.6 all-to-all-done
  427.2 4.5 collective-permute-start.1
  440.1 4.9 all-to-all-start
  447.7 4.6 all-to-all-done
  461.0 4.5 collective-permute-start.1
  473.8 4.9 all-to-all-start
  481.5 4.6 all-to-all-done
  (794 shorter events, 213.3 us)
Async XLA Ops:
  5.3 14.8 %all-to-all-start.1 = ((s32[2,32,256]{2,0,1:T(2,128)}), s32[2,32,256]{2,0,1:T(2,128)S(1)}, u32[]{:S(2)}, u32[]{:S(2)}) async-start(s32[2,32,256]{2,0,1:T(2,128)} %copy.60), calls=%async_computation.1 | async-start | bytes 131072 | tf_op jit(solution)/shard_map/all_to_all | solution.py:166
  20.7 33.6 %collective-permute-start = (f32[1,16,128]{2,1,0:T(8,128)S(1)}, f32[1,16,128]{2,1,0:T(8,128)S(1)}, u32[]{:S(2)}, u32[]{:S(2)}) collective-permute-start(f32[1,16,128]{2,1,0:T(8,128)S(1)} %get-tuple-element.600), channel_id=1, source_target_pairs={{4,0},{8,4},{12,8},{16,12},{20,16},{24,20},{28,24},{5,1},{9,5},{13... | collective-permute-start | bytes 24584 | tf_op jit(solution)/shard_map/while/body/eval_jaxpr/ppermute | solution.py:15
  22.0 32.3 %collective-permute-start.1 = (f32[1,16,128]{2,1,0:T(8,128)S(1)}, f32[1,16,128]{2,1,0:T(8,128)S(1)}, u32[]{:S(2)}, u32[]{:S(2)}) collective-permute-start(f32[1,16,128]{2,1,0:T(8,128)S(1)} %get-tuple-element.603), channel_id=1, source_target_pairs={{0,4},{4,8},{8,12},{12,16},{16,20},{20,24},{24,28},{1,5},{5,9},{9,... | collective-permute-start | bytes 24584 | tf_op jit(solution)/shard_map/while/body/eval_jaxpr/ppermute | solution.py:15
  26.8 15.5 %collective-permute-start.3 = (f32[5,128]{1,0:T(8,128)S(1)}, f32[5,128]{1,0:T(8,128)S(1)}, u32[]{:S(2)}, u32[]{:S(2)}) collective-permute-start(f32[5,128]{1,0:T(8,128)S(1)} %pad_maximum_fusion.8), channel_id=1, source_target_pairs={{0,1},{1,2},{2,3},{4,5},{5,6},{6,7},{8,9},{9,10},{10,11},{12,13},{... | collective-permute-start | bytes 7688 | tf_op jit(solution)/shard_map/while/body/eval_jaxpr/ppermute | solution.py:15
  28.3 14.1 %collective-permute-start.2 = (f32[5,128]{1,0:T(8,128)S(1)}, f32[5,128]{1,0:T(8,128)S(1)}, u32[]{:S(2)}, u32[]{:S(2)}) collective-permute-start(f32[5,128]{1,0:T(8,128)S(1)} %pad_maximum_fusion.7), channel_id=1, source_target_pairs={{1,0},{2,1},{3,2},{5,4},{6,5},{7,6},{9,8},{10,9},{11,10},{13,12},{... | collective-permute-start | bytes 7688 | tf_op jit(solution)/shard_map/while/body/eval_jaxpr/ppermute | solution.py:15
  34.9 12.3 %all-to-all-start = ((f32[2,32,256]{2,0,1:T(2,128)}), f32[2,32,256]{2,0,1:T(2,128)S(1)}, u32[]{:S(2)}, u32[]{:S(2)}) async-start(f32[2,32,256]{2,0,1:T(2,128)} %pad_maximum_fusion.6), calls=%async_computation | async-start | bytes 131072 | tf_op jit(solution)/shard_map/while/body/eval_jaxpr/all_to_all | solution.py:112
  54.5 33.6 %collective-permute-start = (f32[1,16,128]{2,1,0:T(8,128)S(1)}, f32[1,16,128]{2,1,0:T(8,128)S(1)}, u32[]{:S(2)}, u32[]{:S(2)}) collective-permute-start(f32[1,16,128]{2,1,0:T(8,128)S(1)} %get-tuple-element.600), channel_id=1, source_target_pairs={{4,0},{8,4},{12,8},{16,12},{20,16},{24,20},{28,24},{5,1},{9,5},{13... | collective-permute-start | bytes 24584 | tf_op jit(solution)/shard_map/while/body/eval_jaxpr/ppermute | solution.py:15
  55.8 32.3 %collective-permute-start.1 = (f32[1,16,128]{2,1,0:T(8,128)S(1)}, f32[1,16,128]{2,1,0:T(8,128)S(1)}, u32[]{:S(2)}, u32[]{:S(2)}) collective-permute-start(f32[1,16,128]{2,1,0:T(8,128)S(1)} %get-tuple-element.603), channel_id=1, source_target_pairs={{0,4},{4,8},{8,12},{12,16},{16,20},{20,24},{24,28},{1,5},{5,9},{9,... | collective-permute-start | bytes 24584 | tf_op jit(solution)/shard_map/while/body/eval_jaxpr/ppermute | solution.py:15
  60.6 15.5 %collective-permute-start.3 = (f32[5,128]{1,0:T(8,128)S(1)}, f32[5,128]{1,0:T(8,128)S(1)}, u32[]{:S(2)}, u32[]{:S(2)}) collective-permute-start(f32[5,128]{1,0:T(8,128)S(1)} %pad_maximum_fusion.8), channel_id=1, source_target_pairs={{0,1},{1,2},{2,3},{4,5},{5,6},{6,7},{8,9},{9,10},{10,11},{12,13},{... | collective-permute-start | bytes 7688 | tf_op jit(solution)/shard_map/while/body/eval_jaxpr/ppermute | solution.py:15
  62.1 14.1 %collective-permute-start.2 = (f32[5,128]{1,0:T(8,128)S(1)}, f32[5,128]{1,0:T(8,128)S(1)}, u32[]{:S(2)}, u32[]{:S(2)}) collective-permute-start(f32[5,128]{1,0:T(8,128)S(1)} %pad_maximum_fusion.7), channel_id=1, source_target_pairs={{1,0},{2,1},{3,2},{5,4},{6,5},{7,6},{9,8},{10,9},{11,10},{13,12},{... | collective-permute-start | bytes 7688 | tf_op jit(solution)/shard_map/while/body/eval_jaxpr/ppermute | solution.py:15
  68.6 12.3 %all-to-all-start = ((f32[2,32,256]{2,0,1:T(2,128)}), f32[2,32,256]{2,0,1:T(2,128)S(1)}, u32[]{:S(2)}, u32[]{:S(2)}) async-start(f32[2,32,256]{2,0,1:T(2,128)} %pad_maximum_fusion.6), calls=%async_computation | async-start | bytes 131072 | tf_op jit(solution)/shard_map/while/body/eval_jaxpr/all_to_all | solution.py:112
  88.2 33.6 %collective-permute-start = (f32[1,16,128]{2,1,0:T(8,128)S(1)}, f32[1,16,128]{2,1,0:T(8,128)S(1)}, u32[]{:S(2)}, u32[]{:S(2)}) collective-permute-start(f32[1,16,128]{2,1,0:T(8,128)S(1)} %get-tuple-element.600), channel_id=1, source_target_pairs={{4,0},{8,4},{12,8},{16,12},{20,16},{24,20},{28,24},{5,1},{9,5},{13... | collective-permute-start | bytes 24584 | tf_op jit(solution)/shard_map/while/body/eval_jaxpr/ppermute | solution.py:15
  89.5 32.3 %collective-permute-start.1 = (f32[1,16,128]{2,1,0:T(8,128)S(1)}, f32[1,16,128]{2,1,0:T(8,128)S(1)}, u32[]{:S(2)}, u32[]{:S(2)}) collective-permute-start(f32[1,16,128]{2,1,0:T(8,128)S(1)} %get-tuple-element.603), channel_id=1, source_target_pairs={{0,4},{4,8},{8,12},{12,16},{16,20},{20,24},{24,28},{1,5},{5,9},{9,... | collective-permute-start | bytes 24584 | tf_op jit(solution)/shard_map/while/body/eval_jaxpr/ppermute | solution.py:15
  94.3 15.5 %collective-permute-start.3 = (f32[5,128]{1,0:T(8,128)S(1)}, f32[5,128]{1,0:T(8,128)S(1)}, u32[]{:S(2)}, u32[]{:S(2)}) collective-permute-start(f32[5,128]{1,0:T(8,128)S(1)} %pad_maximum_fusion.8), channel_id=1, source_target_pairs={{0,1},{1,2},{2,3},{4,5},{5,6},{6,7},{8,9},{9,10},{10,11},{12,13},{... | collective-permute-start | bytes 7688 | tf_op jit(solution)/shard_map/while/body/eval_jaxpr/ppermute | solution.py:15
  95.8 14.1 %collective-permute-start.2 = (f32[5,128]{1,0:T(8,128)S(1)}, f32[5,128]{1,0:T(8,128)S(1)}, u32[]{:S(2)}, u32[]{:S(2)}) collective-permute-start(f32[5,128]{1,0:T(8,128)S(1)} %pad_maximum_fusion.7), channel_id=1, source_target_pairs={{1,0},{2,1},{3,2},{5,4},{6,5},{7,6},{9,8},{10,9},{11,10},{13,12},{... | collective-permute-start | bytes 7688 | tf_op jit(solution)/shard_map/while/body/eval_jaxpr/ppermute | solution.py:15
  102.4 12.3 %all-to-all-start = ((f32[2,32,256]{2,0,1:T(2,128)}), f32[2,32,256]{2,0,1:T(2,128)S(1)}, u32[]{:S(2)}, u32[]{:S(2)}) async-start(f32[2,32,256]{2,0,1:T(2,128)} %pad_maximum_fusion.6), calls=%async_computation | async-start | bytes 131072 | tf_op jit(solution)/shard_map/while/body/eval_jaxpr/all_to_all | solution.py:112
  122.0 33.6 %collective-permute-start = (f32[1,16,128]{2,1,0:T(8,128)S(1)}, f32[1,16,128]{2,1,0:T(8,128)S(1)}, u32[]{:S(2)}, u32[]{:S(2)}) collective-permute-start(f32[1,16,128]{2,1,0:T(8,128)S(1)} %get-tuple-element.600), channel_id=1, source_target_pairs={{4,0},{8,4},{12,8},{16,12},{20,16},{24,20},{28,24},{5,1},{9,5},{13... | collective-permute-start | bytes 24584 | tf_op jit(solution)/shard_map/while/body/eval_jaxpr/ppermute | solution.py:15
  123.3 32.3 %collective-permute-start.1 = (f32[1,16,128]{2,1,0:T(8,128)S(1)}, f32[1,16,128]{2,1,0:T(8,128)S(1)}, u32[]{:S(2)}, u32[]{:S(2)}) collective-permute-start(f32[1,16,128]{2,1,0:T(8,128)S(1)} %get-tuple-element.603), channel_id=1, source_target_pairs={{0,4},{4,8},{8,12},{12,16},{16,20},{20,24},{24,28},{1,5},{5,9},{9,... | collective-permute-start | bytes 24584 | tf_op jit(solution)/shard_map/while/body/eval_jaxpr/ppermute | solution.py:15
  128.1 15.5 %collective-permute-start.3 = (f32[5,128]{1,0:T(8,128)S(1)}, f32[5,128]{1,0:T(8,128)S(1)}, u32[]{:S(2)}, u32[]{:S(2)}) collective-permute-start(f32[5,128]{1,0:T(8,128)S(1)} %pad_maximum_fusion.8), channel_id=1, source_target_pairs={{0,1},{1,2},{2,3},{4,5},{5,6},{6,7},{8,9},{9,10},{10,11},{12,13},{... | collective-permute-start | bytes 7688 | tf_op jit(solution)/shard_map/while/body/eval_jaxpr/ppermute | solution.py:15
  129.6 14.1 %collective-permute-start.2 = (f32[5,128]{1,0:T(8,128)S(1)}, f32[5,128]{1,0:T(8,128)S(1)}, u32[]{:S(2)}, u32[]{:S(2)}) collective-permute-start(f32[5,128]{1,0:T(8,128)S(1)} %pad_maximum_fusion.7), channel_id=1, source_target_pairs={{1,0},{2,1},{3,2},{5,4},{6,5},{7,6},{9,8},{10,9},{11,10},{13,12},{... | collective-permute-start | bytes 7688 | tf_op jit(solution)/shard_map/while/body/eval_jaxpr/ppermute | solution.py:15
  136.2 12.3 %all-to-all-start = ((f32[2,32,256]{2,0,1:T(2,128)}), f32[2,32,256]{2,0,1:T(2,128)S(1)}, u32[]{:S(2)}, u32[]{:S(2)}) async-start(f32[2,32,256]{2,0,1:T(2,128)} %pad_maximum_fusion.6), calls=%async_computation | async-start | bytes 131072 | tf_op jit(solution)/shard_map/while/body/eval_jaxpr/all_to_all | solution.py:112
  155.8 33.6 %collective-permute-start = (f32[1,16,128]{2,1,0:T(8,128)S(1)}, f32[1,16,128]{2,1,0:T(8,128)S(1)}, u32[]{:S(2)}, u32[]{:S(2)}) collective-permute-start(f32[1,16,128]{2,1,0:T(8,128)S(1)} %get-tuple-element.600), channel_id=1, source_target_pairs={{4,0},{8,4},{12,8},{16,12},{20,16},{24,20},{28,24},{5,1},{9,5},{13... | collective-permute-start | bytes 24584 | tf_op jit(solution)/shard_map/while/body/eval_jaxpr/ppermute | solution.py:15
  157.1 32.3 %collective-permute-start.1 = (f32[1,16,128]{2,1,0:T(8,128)S(1)}, f32[1,16,128]{2,1,0:T(8,128)S(1)}, u32[]{:S(2)}, u32[]{:S(2)}) collective-permute-start(f32[1,16,128]{2,1,0:T(8,128)S(1)} %get-tuple-element.603), channel_id=1, source_target_pairs={{0,4},{4,8},{8,12},{12,16},{16,20},{20,24},{24,28},{1,5},{5,9},{9,... | collective-permute-start | bytes 24584 | tf_op jit(solution)/shard_map/while/body/eval_jaxpr/ppermute | solution.py:15
  161.9 15.5 %collective-permute-start.3 = (f32[5,128]{1,0:T(8,128)S(1)}, f32[5,128]{1,0:T(8,128)S(1)}, u32[]{:S(2)}, u32[]{:S(2)}) collective-permute-start(f32[5,128]{1,0:T(8,128)S(1)} %pad_maximum_fusion.8), channel_id=1, source_target_pairs={{0,1},{1,2},{2,3},{4,5},{5,6},{6,7},{8,9},{9,10},{10,11},{12,13},{... | collective-permute-start | bytes 7688 | tf_op jit(solution)/shard_map/while/body/eval_jaxpr/ppermute | solution.py:15
  163.4 14.1 %collective-permute-start.2 = (f32[5,128]{1,0:T(8,128)S(1)}, f32[5,128]{1,0:T(8,128)S(1)}, u32[]{:S(2)}, u32[]{:S(2)}) collective-permute-start(f32[5,128]{1,0:T(8,128)S(1)} %pad_maximum_fusion.7), channel_id=1, source_target_pairs={{1,0},{2,1},{3,2},{5,4},{6,5},{7,6},{9,8},{10,9},{11,10},{13,12},{... | collective-permute-start | bytes 7688 | tf_op jit(solution)/shard_map/while/body/eval_jaxpr/ppermute | solution.py:15
  169.9 12.3 %all-to-all-start = ((f32[2,32,256]{2,0,1:T(2,128)}), f32[2,32,256]{2,0,1:T(2,128)S(1)}, u32[]{:S(2)}, u32[]{:S(2)}) async-start(f32[2,32,256]{2,0,1:T(2,128)} %pad_maximum_fusion.6), calls=%async_computation | async-start | bytes 131072 | tf_op jit(solution)/shard_map/while/body/eval_jaxpr/all_to_all | solution.py:112
  189.5 33.6 %collective-permute-start = (f32[1,16,128]{2,1,0:T(8,128)S(1)}, f32[1,16,128]{2,1,0:T(8,128)S(1)}, u32[]{:S(2)}, u32[]{:S(2)}) collective-permute-start(f32[1,16,128]{2,1,0:T(8,128)S(1)} %get-tuple-element.600), channel_id=1, source_target_pairs={{4,0},{8,4},{12,8},{16,12},{20,16},{24,20},{28,24},{5,1},{9,5},{13... | collective-permute-start | bytes 24584 | tf_op jit(solution)/shard_map/while/body/eval_jaxpr/ppermute | solution.py:15
  190.8 32.3 %collective-permute-start.1 = (f32[1,16,128]{2,1,0:T(8,128)S(1)}, f32[1,16,128]{2,1,0:T(8,128)S(1)}, u32[]{:S(2)}, u32[]{:S(2)}) collective-permute-start(f32[1,16,128]{2,1,0:T(8,128)S(1)} %get-tuple-element.603), channel_id=1, source_target_pairs={{0,4},{4,8},{8,12},{12,16},{16,20},{20,24},{24,28},{1,5},{5,9},{9,... | collective-permute-start | bytes 24584 | tf_op jit(solution)/shard_map/while/body/eval_jaxpr/ppermute | solution.py:15
  195.6 15.5 %collective-permute-start.3 = (f32[5,128]{1,0:T(8,128)S(1)}, f32[5,128]{1,0:T(8,128)S(1)}, u32[]{:S(2)}, u32[]{:S(2)}) collective-permute-start(f32[5,128]{1,0:T(8,128)S(1)} %pad_maximum_fusion.8), channel_id=1, source_target_pairs={{0,1},{1,2},{2,3},{4,5},{5,6},{6,7},{8,9},{9,10},{10,11},{12,13},{... | collective-permute-start | bytes 7688 | tf_op jit(solution)/shard_map/while/body/eval_jaxpr/ppermute | solution.py:15
  197.1 14.1 %collective-permute-start.2 = (f32[5,128]{1,0:T(8,128)S(1)}, f32[5,128]{1,0:T(8,128)S(1)}, u32[]{:S(2)}, u32[]{:S(2)}) collective-permute-start(f32[5,128]{1,0:T(8,128)S(1)} %pad_maximum_fusion.7), channel_id=1, source_target_pairs={{1,0},{2,1},{3,2},{5,4},{6,5},{7,6},{9,8},{10,9},{11,10},{13,12},{... | collective-permute-start | bytes 7688 | tf_op jit(solution)/shard_map/while/body/eval_jaxpr/ppermute | solution.py:15
  203.7 12.3 %all-to-all-start = ((f32[2,32,256]{2,0,1:T(2,128)}), f32[2,32,256]{2,0,1:T(2,128)S(1)}, u32[]{:S(2)}, u32[]{:S(2)}) async-start(f32[2,32,256]{2,0,1:T(2,128)} %pad_maximum_fusion.6), calls=%async_computation | async-start | bytes 131072 | tf_op jit(solution)/shard_map/while/body/eval_jaxpr/all_to_all | solution.py:112
  223.3 33.6 %collective-permute-start = (f32[1,16,128]{2,1,0:T(8,128)S(1)}, f32[1,16,128]{2,1,0:T(8,128)S(1)}, u32[]{:S(2)}, u32[]{:S(2)}) collective-permute-start(f32[1,16,128]{2,1,0:T(8,128)S(1)} %get-tuple-element.600), channel_id=1, source_target_pairs={{4,0},{8,4},{12,8},{16,12},{20,16},{24,20},{28,24},{5,1},{9,5},{13... | collective-permute-start | bytes 24584 | tf_op jit(solution)/shard_map/while/body/eval_jaxpr/ppermute | solution.py:15
  224.6 32.3 %collective-permute-start.1 = (f32[1,16,128]{2,1,0:T(8,128)S(1)}, f32[1,16,128]{2,1,0:T(8,128)S(1)}, u32[]{:S(2)}, u32[]{:S(2)}) collective-permute-start(f32[1,16,128]{2,1,0:T(8,128)S(1)} %get-tuple-element.603), channel_id=1, source_target_pairs={{0,4},{4,8},{8,12},{12,16},{16,20},{20,24},{24,28},{1,5},{5,9},{9,... | collective-permute-start | bytes 24584 | tf_op jit(solution)/shard_map/while/body/eval_jaxpr/ppermute | solution.py:15
  229.4 15.5 %collective-permute-start.3 = (f32[5,128]{1,0:T(8,128)S(1)}, f32[5,128]{1,0:T(8,128)S(1)}, u32[]{:S(2)}, u32[]{:S(2)}) collective-permute-start(f32[5,128]{1,0:T(8,128)S(1)} %pad_maximum_fusion.8), channel_id=1, source_target_pairs={{0,1},{1,2},{2,3},{4,5},{5,6},{6,7},{8,9},{9,10},{10,11},{12,13},{... | collective-permute-start | bytes 7688 | tf_op jit(solution)/shard_map/while/body/eval_jaxpr/ppermute | solution.py:15
  230.9 14.1 %collective-permute-start.2 = (f32[5,128]{1,0:T(8,128)S(1)}, f32[5,128]{1,0:T(8,128)S(1)}, u32[]{:S(2)}, u32[]{:S(2)}) collective-permute-start(f32[5,128]{1,0:T(8,128)S(1)} %pad_maximum_fusion.7), channel_id=1, source_target_pairs={{1,0},{2,1},{3,2},{5,4},{6,5},{7,6},{9,8},{10,9},{11,10},{13,12},{... | collective-permute-start | bytes 7688 | tf_op jit(solution)/shard_map/while/body/eval_jaxpr/ppermute | solution.py:15
  237.5 12.3 %all-to-all-start = ((f32[2,32,256]{2,0,1:T(2,128)}), f32[2,32,256]{2,0,1:T(2,128)S(1)}, u32[]{:S(2)}, u32[]{:S(2)}) async-start(f32[2,32,256]{2,0,1:T(2,128)} %pad_maximum_fusion.6), calls=%async_computation | async-start | bytes 131072 | tf_op jit(solution)/shard_map/while/body/eval_jaxpr/all_to_all | solution.py:112
  257.1 33.6 %collective-permute-start = (f32[1,16,128]{2,1,0:T(8,128)S(1)}, f32[1,16,128]{2,1,0:T(8,128)S(1)}, u32[]{:S(2)}, u32[]{:S(2)}) collective-permute-start(f32[1,16,128]{2,1,0:T(8,128)S(1)} %get-tuple-element.600), channel_id=1, source_target_pairs={{4,0},{8,4},{12,8},{16,12},{20,16},{24,20},{28,24},{5,1},{9,5},{13... | collective-permute-start | bytes 24584 | tf_op jit(solution)/shard_map/while/body/eval_jaxpr/ppermute | solution.py:15
  258.4 32.3 %collective-permute-start.1 = (f32[1,16,128]{2,1,0:T(8,128)S(1)}, f32[1,16,128]{2,1,0:T(8,128)S(1)}, u32[]{:S(2)}, u32[]{:S(2)}) collective-permute-start(f32[1,16,128]{2,1,0:T(8,128)S(1)} %get-tuple-element.603), channel_id=1, source_target_pairs={{0,4},{4,8},{8,12},{12,16},{16,20},{20,24},{24,28},{1,5},{5,9},{9,... | collective-permute-start | bytes 24584 | tf_op jit(solution)/shard_map/while/body/eval_jaxpr/ppermute | solution.py:15
  263.2 15.5 %collective-permute-start.3 = (f32[5,128]{1,0:T(8,128)S(1)}, f32[5,128]{1,0:T(8,128)S(1)}, u32[]{:S(2)}, u32[]{:S(2)}) collective-permute-start(f32[5,128]{1,0:T(8,128)S(1)} %pad_maximum_fusion.8), channel_id=1, source_target_pairs={{0,1},{1,2},{2,3},{4,5},{5,6},{6,7},{8,9},{9,10},{10,11},{12,13},{... | collective-permute-start | bytes 7688 | tf_op jit(solution)/shard_map/while/body/eval_jaxpr/ppermute | solution.py:15
  264.7 14.1 %collective-permute-start.2 = (f32[5,128]{1,0:T(8,128)S(1)}, f32[5,128]{1,0:T(8,128)S(1)}, u32[]{:S(2)}, u32[]{:S(2)}) collective-permute-start(f32[5,128]{1,0:T(8,128)S(1)} %pad_maximum_fusion.7), channel_id=1, source_target_pairs={{1,0},{2,1},{3,2},{5,4},{6,5},{7,6},{9,8},{10,9},{11,10},{13,12},{... | collective-permute-start | bytes 7688 | tf_op jit(solution)/shard_map/while/body/eval_jaxpr/ppermute | solution.py:15
  290.8 33.6 %collective-permute-start = (f32[1,16,128]{2,1,0:T(8,128)S(1)}, f32[1,16,128]{2,1,0:T(8,128)S(1)}, u32[]{:S(2)}, u32[]{:S(2)}) collective-permute-start(f32[1,16,128]{2,1,0:T(8,128)S(1)} %get-tuple-element.600), channel_id=1, source_target_pairs={{4,0},{8,4},{12,8},{16,12},{20,16},{24,20},{28,24},{5,1},{9,5},{13... | collective-permute-start | bytes 24584 | tf_op jit(solution)/shard_map/while/body/eval_jaxpr/ppermute | solution.py:15
  292.1 32.3 %collective-permute-start.1 = (f32[1,16,128]{2,1,0:T(8,128)S(1)}, f32[1,16,128]{2,1,0:T(8,128)S(1)}, u32[]{:S(2)}, u32[]{:S(2)}) collective-permute-start(f32[1,16,128]{2,1,0:T(8,128)S(1)} %get-tuple-element.603), channel_id=1, source_target_pairs={{0,4},{4,8},{8,12},{12,16},{16,20},{20,24},{24,28},{1,5},{5,9},{9,... | collective-permute-start | bytes 24584 | tf_op jit(solution)/shard_map/while/body/eval_jaxpr/ppermute | solution.py:15
  296.9 15.5 %collective-permute-start.3 = (f32[5,128]{1,0:T(8,128)S(1)}, f32[5,128]{1,0:T(8,128)S(1)}, u32[]{:S(2)}, u32[]{:S(2)}) collective-permute-start(f32[5,128]{1,0:T(8,128)S(1)} %pad_maximum_fusion.8), channel_id=1, source_target_pairs={{0,1},{1,2},{2,3},{4,5},{5,6},{6,7},{8,9},{9,10},{10,11},{12,13},{... | collective-permute-start | bytes 7688 | tf_op jit(solution)/shard_map/while/body/eval_jaxpr/ppermute | solution.py:15
  298.4 14.1 %collective-permute-start.2 = (f32[5,128]{1,0:T(8,128)S(1)}, f32[5,128]{1,0:T(8,128)S(1)}, u32[]{:S(2)}, u32[]{:S(2)}) collective-permute-start(f32[5,128]{1,0:T(8,128)S(1)} %pad_maximum_fusion.7), channel_id=1, source_target_pairs={{1,0},{2,1},{3,2},{5,4},{6,5},{7,6},{9,8},{10,9},{11,10},{13,12},{... | collective-permute-start | bytes 7688 | tf_op jit(solution)/shard_map/while/body/eval_jaxpr/ppermute | solution.py:15
  324.6 33.6 %collective-permute-start = (f32[1,16,128]{2,1,0:T(8,128)S(1)}, f32[1,16,128]{2,1,0:T(8,128)S(1)}, u32[]{:S(2)}, u32[]{:S(2)}) collective-permute-start(f32[1,16,128]{2,1,0:T(8,128)S(1)} %get-tuple-element.600), channel_id=1, source_target_pairs={{4,0},{8,4},{12,8},{16,12},{20,16},{24,20},{28,24},{5,1},{9,5},{13... | collective-permute-start | bytes 24584 | tf_op jit(solution)/shard_map/while/body/eval_jaxpr/ppermute | solution.py:15
  325.9 32.3 %collective-permute-start.1 = (f32[1,16,128]{2,1,0:T(8,128)S(1)}, f32[1,16,128]{2,1,0:T(8,128)S(1)}, u32[]{:S(2)}, u32[]{:S(2)}) collective-permute-start(f32[1,16,128]{2,1,0:T(8,128)S(1)} %get-tuple-element.603), channel_id=1, source_target_pairs={{0,4},{4,8},{8,12},{12,16},{16,20},{20,24},{24,28},{1,5},{5,9},{9,... | collective-permute-start | bytes 24584 | tf_op jit(solution)/shard_map/while/body/eval_jaxpr/ppermute | solution.py:15
  330.7 15.5 %collective-permute-start.3 = (f32[5,128]{1,0:T(8,128)S(1)}, f32[5,128]{1,0:T(8,128)S(1)}, u32[]{:S(2)}, u32[]{:S(2)}) collective-permute-start(f32[5,128]{1,0:T(8,128)S(1)} %pad_maximum_fusion.8), channel_id=1, source_target_pairs={{0,1},{1,2},{2,3},{4,5},{5,6},{6,7},{8,9},{9,10},{10,11},{12,13},{... | collective-permute-start | bytes 7688 | tf_op jit(solution)/shard_map/while/body/eval_jaxpr/ppermute | solution.py:15
  332.2 14.1 %collective-permute-start.2 = (f32[5,128]{1,0:T(8,128)S(1)}, f32[5,128]{1,0:T(8,128)S(1)}, u32[]{:S(2)}, u32[]{:S(2)}) collective-permute-start(f32[5,128]{1,0:T(8,128)S(1)} %pad_maximum_fusion.7), channel_id=1, source_target_pairs={{1,0},{2,1},{3,2},{5,4},{6,5},{7,6},{9,8},{10,9},{11,10},{13,12},{... | collective-permute-start | bytes 7688 | tf_op jit(solution)/shard_map/while/body/eval_jaxpr/ppermute | solution.py:15
  358.4 33.6 %collective-permute-start = (f32[1,16,128]{2,1,0:T(8,128)S(1)}, f32[1,16,128]{2,1,0:T(8,128)S(1)}, u32[]{:S(2)}, u32[]{:S(2)}) collective-permute-start(f32[1,16,128]{2,1,0:T(8,128)S(1)} %get-tuple-element.600), channel_id=1, source_target_pairs={{4,0},{8,4},{12,8},{16,12},{20,16},{24,20},{28,24},{5,1},{9,5},{13... | collective-permute-start | bytes 24584 | tf_op jit(solution)/shard_map/while/body/eval_jaxpr/ppermute | solution.py:15
  359.7 32.3 %collective-permute-start.1 = (f32[1,16,128]{2,1,0:T(8,128)S(1)}, f32[1,16,128]{2,1,0:T(8,128)S(1)}, u32[]{:S(2)}, u32[]{:S(2)}) collective-permute-start(f32[1,16,128]{2,1,0:T(8,128)S(1)} %get-tuple-element.603), channel_id=1, source_target_pairs={{0,4},{4,8},{8,12},{12,16},{16,20},{20,24},{24,28},{1,5},{5,9},{9,... | collective-permute-start | bytes 24584 | tf_op jit(solution)/shard_map/while/body/eval_jaxpr/ppermute | solution.py:15
  364.5 15.5 %collective-permute-start.3 = (f32[5,128]{1,0:T(8,128)S(1)}, f32[5,128]{1,0:T(8,128)S(1)}, u32[]{:S(2)}, u32[]{:S(2)}) collective-permute-start(f32[5,128]{1,0:T(8,128)S(1)} %pad_maximum_fusion.8), channel_id=1, source_target_pairs={{0,1},{1,2},{2,3},{4,5},{5,6},{6,7},{8,9},{9,10},{10,11},{12,13},{... | collective-permute-start | bytes 7688 | tf_op jit(solution)/shard_map/while/body/eval_jaxpr/ppermute | solution.py:15
  366.0 14.1 %collective-permute-start.2 = (f32[5,128]{1,0:T(8,128)S(1)}, f32[5,128]{1,0:T(8,128)S(1)}, u32[]{:S(2)}, u32[]{:S(2)}) collective-permute-start(f32[5,128]{1,0:T(8,128)S(1)} %pad_maximum_fusion.7), channel_id=1, source_target_pairs={{1,0},{2,1},{3,2},{5,4},{6,5},{7,6},{9,8},{10,9},{11,10},{13,12},{... | collective-permute-start | bytes 7688 | tf_op jit(solution)/shard_map/while/body/eval_jaxpr/ppermute | solution.py:15
  392.1 33.6 %collective-permute-start = (f32[1,16,128]{2,1,0:T(8,128)S(1)}, f32[1,16,128]{2,1,0:T(8,128)S(1)}, u32[]{:S(2)}, u32[]{:S(2)}) collective-permute-start(f32[1,16,128]{2,1,0:T(8,128)S(1)} %get-tuple-element.600), channel_id=1, source_target_pairs={{4,0},{8,4},{12,8},{16,12},{20,16},{24,20},{28,24},{5,1},{9,5},{13... | collective-permute-start | bytes 24584 | tf_op jit(solution)/shard_map/while/body/eval_jaxpr/ppermute | solution.py:15
  393.4 32.3 %collective-permute-start.1 = (f32[1,16,128]{2,1,0:T(8,128)S(1)}, f32[1,16,128]{2,1,0:T(8,128)S(1)}, u32[]{:S(2)}, u32[]{:S(2)}) collective-permute-start(f32[1,16,128]{2,1,0:T(8,128)S(1)} %get-tuple-element.603), channel_id=1, source_target_pairs={{0,4},{4,8},{8,12},{12,16},{16,20},{20,24},{24,28},{1,5},{5,9},{9,... | collective-permute-start | bytes 24584 | tf_op jit(solution)/shard_map/while/body/eval_jaxpr/ppermute | solution.py:15
  398.2 15.5 %collective-permute-start.3 = (f32[5,128]{1,0:T(8,128)S(1)}, f32[5,128]{1,0:T(8,128)S(1)}, u32[]{:S(2)}, u32[]{:S(2)}) collective-permute-start(f32[5,128]{1,0:T(8,128)S(1)} %pad_maximum_fusion.8), channel_id=1, source_target_pairs={{0,1},{1,2},{2,3},{4,5},{5,6},{6,7},{8,9},{9,10},{10,11},{12,13},{... | collective-permute-start | bytes 7688 | tf_op jit(solution)/shard_map/while/body/eval_jaxpr/ppermute | solution.py:15
  399.7 14.1 %collective-permute-start.2 = (f32[5,128]{1,0:T(8,128)S(1)}, f32[5,128]{1,0:T(8,128)S(1)}, u32[]{:S(2)}, u32[]{:S(2)}) collective-permute-start(f32[5,128]{1,0:T(8,128)S(1)} %pad_maximum_fusion.7), channel_id=1, source_target_pairs={{1,0},{2,1},{3,2},{5,4},{6,5},{7,6},{9,8},{10,9},{11,10},{13,12},{... | collective-permute-start | bytes 7688 | tf_op jit(solution)/shard_map/while/body/eval_jaxpr/ppermute | solution.py:15
  425.9 33.6 %collective-permute-start = (f32[1,16,128]{2,1,0:T(8,128)S(1)}, f32[1,16,128]{2,1,0:T(8,128)S(1)}, u32[]{:S(2)}, u32[]{:S(2)}) collective-permute-start(f32[1,16,128]{2,1,0:T(8,128)S(1)} %get-tuple-element.600), channel_id=1, source_target_pairs={{4,0},{8,4},{12,8},{16,12},{20,16},{24,20},{28,24},{5,1},{9,5},{13... | collective-permute-start | bytes 24584 | tf_op jit(solution)/shard_map/while/body/eval_jaxpr/ppermute | solution.py:15
  427.2 32.3 %collective-permute-start.1 = (f32[1,16,128]{2,1,0:T(8,128)S(1)}, f32[1,16,128]{2,1,0:T(8,128)S(1)}, u32[]{:S(2)}, u32[]{:S(2)}) collective-permute-start(f32[1,16,128]{2,1,0:T(8,128)S(1)} %get-tuple-element.603), channel_id=1, source_target_pairs={{0,4},{4,8},{8,12},{12,16},{16,20},{20,24},{24,28},{1,5},{5,9},{9,... | collective-permute-start | bytes 24584 | tf_op jit(solution)/shard_map/while/body/eval_jaxpr/ppermute | solution.py:15
  432.0 15.5 %collective-permute-start.3 = (f32[5,128]{1,0:T(8,128)S(1)}, f32[5,128]{1,0:T(8,128)S(1)}, u32[]{:S(2)}, u32[]{:S(2)}) collective-permute-start(f32[5,128]{1,0:T(8,128)S(1)} %pad_maximum_fusion.8), channel_id=1, source_target_pairs={{0,1},{1,2},{2,3},{4,5},{5,6},{6,7},{8,9},{9,10},{10,11},{12,13},{... | collective-permute-start | bytes 7688 | tf_op jit(solution)/shard_map/while/body/eval_jaxpr/ppermute | solution.py:15
  433.5 14.1 %collective-permute-start.2 = (f32[5,128]{1,0:T(8,128)S(1)}, f32[5,128]{1,0:T(8,128)S(1)}, u32[]{:S(2)}, u32[]{:S(2)}) collective-permute-start(f32[5,128]{1,0:T(8,128)S(1)} %pad_maximum_fusion.7), channel_id=1, source_target_pairs={{1,0},{2,1},{3,2},{5,4},{6,5},{7,6},{9,8},{10,9},{11,10},{13,12},{... | collective-permute-start | bytes 7688 | tf_op jit(solution)/shard_map/while/body/eval_jaxpr/ppermute | solution.py:15
  459.7 33.6 %collective-permute-start = (f32[1,16,128]{2,1,0:T(8,128)S(1)}, f32[1,16,128]{2,1,0:T(8,128)S(1)}, u32[]{:S(2)}, u32[]{:S(2)}) collective-permute-start(f32[1,16,128]{2,1,0:T(8,128)S(1)} %get-tuple-element.600), channel_id=1, source_target_pairs={{4,0},{8,4},{12,8},{16,12},{20,16},{24,20},{28,24},{5,1},{9,5},{13... | collective-permute-start | bytes 24584 | tf_op jit(solution)/shard_map/while/body/eval_jaxpr/ppermute | solution.py:15
  461.0 32.3 %collective-permute-start.1 = (f32[1,16,128]{2,1,0:T(8,128)S(1)}, f32[1,16,128]{2,1,0:T(8,128)S(1)}, u32[]{:S(2)}, u32[]{:S(2)}) collective-permute-start(f32[1,16,128]{2,1,0:T(8,128)S(1)} %get-tuple-element.603), channel_id=1, source_target_pairs={{0,4},{4,8},{8,12},{12,16},{16,20},{20,24},{24,28},{1,5},{5,9},{9,... | collective-permute-start | bytes 24584 | tf_op jit(solution)/shard_map/while/body/eval_jaxpr/ppermute | solution.py:15
  465.8 15.5 %collective-permute-start.3 = (f32[5,128]{1,0:T(8,128)S(1)}, f32[5,128]{1,0:T(8,128)S(1)}, u32[]{:S(2)}, u32[]{:S(2)}) collective-permute-start(f32[5,128]{1,0:T(8,128)S(1)} %pad_maximum_fusion.8), channel_id=1, source_target_pairs={{0,1},{1,2},{2,3},{4,5},{5,6},{6,7},{8,9},{9,10},{10,11},{12,13},{... | collective-permute-start | bytes 7688 | tf_op jit(solution)/shard_map/while/body/eval_jaxpr/ppermute | solution.py:15
  467.3 14.1 %collective-permute-start.2 = (f32[5,128]{1,0:T(8,128)S(1)}, f32[5,128]{1,0:T(8,128)S(1)}, u32[]{:S(2)}, u32[]{:S(2)}) collective-permute-start(f32[5,128]{1,0:T(8,128)S(1)} %pad_maximum_fusion.7), channel_id=1, source_target_pairs={{1,0},{2,1},{3,2},{5,4},{6,5},{7,6},{9,8},{10,9},{11,10},{13,12},{... | collective-permute-start | bytes 7688 | tf_op jit(solution)/shard_map/while/body/eval_jaxpr/ppermute | solution.py:15
  (81 other events, 515.6 us)
where the time goes:
time: 496 us; the launch traced here: 494 us
  starting transfers between devices  196 us (40%)
  matrix products  164 us (33%)
  waiting for transfers between devices  70.3 us (14%)
  other arithmetic  47.9 us (10%)
  local copies, waits for them, and re-layouts  10.2 us (2%)
  loops' own time  5.33 us (1%)
    ppermute x56, starting transfers between devices, shift_pair(): return (lax.ppermute(up, axis, forward), lax.ppermute(down, axis, backward))  120 us
    dot_general x28, matrix products, place_split(): lax.dot_general(onehot, weighted.astype(jnp.bfloat16), (((0,), (0,)), (()...  96.1 us
    all_to_all x14, starting transfers between devices, trade_both(): lax.all_to_all(paired, ('slab', 'plane'), split_axis=1, concat_axis=1, ti...  68 us
    all_to_all x14, waiting for transfers between devices, trade_both(): lax.all_to_all(paired, ('slab', 'plane'), split_axis=1, concat_axis=1, ti...  64.9 us
    dot_general x28, matrix products, pick_split(): jnp.dot(onehot.astype(jnp.bfloat16), stacked, preferred_element_type=jnp....  63.1 us
    reduce_sum x28, other arithmetic, membrane(): return (renewed, jnp.sum(driving * renewed, axis=0))  33.5 us
  transfers between devices with their start and end apart: 71, of which 15 were waited for; matrix products, arithmetic and copies ran while one was open for 43% of the time, Pallas kernels for 0%

commit v1 on v0

--- a/solution.py
+++ b/solution.py
@@ -109,7 +109,15 @@
 
 
 def trade_both(paired):
-    return lax.all_to_all(paired, ("slab", "plane"), split_axis=1, concat_axis=1, tiled=True)
+    return jnp.concatenate(
+        lax.all_to_all(
+            jnp.stack(jnp.split(paired, lax.axis_size(("slab", "plane")), axis=1)),
+            ("slab", "plane"),
+            0,
+            0,
+        ),
+        axis=1,
+    )
 
 
 def body(

time: 496 us -> 749 us (1.51)
  local copies, waits for them, and re-layouts: 10.2 us -> 272 us
  other arithmetic: 47.9 us -> 38.2 us
    while x84 -> x532, local copies, waits for them, and re-layouts: 0.41 us -> 254 us
    another operation x42 -> x28, other arithmetic: 9.95 us -> 0.28 us  [the longest x14 9.67 us: advance(): jnp.stack([fibre_at_slot, tissue_at_slot]).reshape(2, devices, capacity)]
    another operation x0 -> x56, local copies, waits for them, and re-layouts: none -> 8.36 us  [the longest x14 7.98 us: trade_both(): jnp.stack(jnp.split(paired, lax.axis_size(('slab', 'plane')), axis=1))]
  transfers between devices with their start and end apart: 71 -> 71, of which waited for: 15 -> 15; matrix products, arithmetic and copies ran while one was open for 43% -> 62% of each run, Pallas kernels for 0% -> 0%
where the time goes in v1:
time: 749 us; the launch traced here: 747 us
  local copies, waits for them, and re-layouts  272 us (36%)
  starting transfers between devices  196 us (26%)
  matrix products  164 us (22%)
  waiting for transfers between devices  70.3 us (9%)
  other arithmetic  38.2 us (5%)
    while x532, local copies, waits for them, and re-layouts  254 us
    ppermute x56, starting transfers between devices, shift_pair(): return (lax.ppermute(up, axis, forward), lax.ppermute(down, axis, backward))  120 us
    dot_general x28, matrix products, place_split(): lax.dot_general(onehot, weighted.astype(jnp.bfloat16), (((0,), (0,)), (()...  96.1 us
    all_to_all x14, starting transfers between devices, trade_both(): lax.all_to_all(jnp.stack(jnp.split(paired, lax.axis_size(('slab', 'plane'...  68.1 us
    all_to_all x14, waiting for transfers between devices, trade_both(): lax.all_to_all(jnp.stack(jnp.split(paired, lax.axis_size(('slab', 'plane'...  64.9 us
    dot_general x28, matrix products, pick_split(): jnp.dot(onehot.astype(jnp.bfloat16), stacked, preferred_element_type=jnp....  63.2 us
    reduce_sum x28, other arithmetic, membrane(): return (renewed, jnp.sum(driving * renewed, axis=0))  33.5 us
  transfers between devices with their start and end apart: 71, of which 15 were waited for; matrix products, arithmetic and copies ran while one was open for 62% of the time, Pallas kernels for 0%

profile of v1, /device:TPU:0, one launch (start us, length us, event | category | flops | bytes accessed | tf_op | source)
XLA Modules:
  0.0 746.9 jit_solution(17975531711647793903)
XLA Ops:
  5.3 7.3 all-to-all-start.1
  14.7 5.3 all-to-all-done.1
  20.5 725.8 %while.20 = (s32[]{:T(128)}, f32[4,16,128]{2,1,0:T(8,128)S(1)}, f32[40,4,16,128]{3,2,1,0:T(8,128)S(1)}, f32[16,512]{1,0:T(8,128)S(1)}, f32[40,16,512]{2,1,0:T(8,...) while((s32[]{:T(128)}, f32[4,16,128]{2,1,0:T(8,128)S(1)}, ...), condition=%wide.region_8.9_spmd.clone, body=%wide.region_3.8_spmd.clone.sunk | while | flops 1107426560 | bytes 8597641 | solution.py:231
  22.0 4.5 collective-permute-start.1
  52.9 4.9 all-to-all-start
  60.6 4.6 all-to-all-done
  65.3 3.4 fusion.179
  68.8 3.4 fusion.173
  73.8 4.5 collective-permute-start.1
  104.8 4.9 all-to-all-start
  112.4 4.6 all-to-all-done
  117.1 3.4 fusion.179
  120.6 3.4 fusion.173
  125.7 4.5 collective-permute-start.1
  156.6 4.9 all-to-all-start
  164.2 4.6 all-to-all-done
  168.9 3.4 fusion.179
  172.4 3.4 fusion.173
  177.5 4.5 collective-permute-start.1
  208.4 4.9 all-to-all-start
  216.1 4.6 all-to-all-done
  220.8 3.4 fusion.179
  224.3 3.4 fusion.173
  229.3 4.5 collective-permute-start.1
  260.3 4.9 all-to-all-start
  267.9 4.6 all-to-all-done
  272.6 3.4 fusion.179
  276.1 3.4 fusion.173
  281.1 4.5 collective-permute-start.1
  312.1 4.9 all-to-all-start
  319.7 4.6 all-to-all-done
  324.4 3.4 fusion.179
  327.9 3.4 fusion.173
  333.0 4.5 collective-permute-start.1
  363.9 4.9 all-to-all-start
  371.5 4.6 all-to-all-done
  376.2 3.4 fusion.179
  379.8 3.4 fusion.173
  384.8 4.5 collective-permute-start.1
  415.7 4.9 all-to-all-start
  423.4 4.6 all-to-all-done
  428.1 3.4 fusion.179
  431.6 3.4 fusion.173
  436.6 4.5 collective-permute-start.1
  467.6 4.9 all-to-all-start
  475.2 4.6 all-to-all-done
  479.9 3.4 fusion.179
  483.4 3.4 fusion.173
  488.4 4.5 collective-permute-start.1
  519.4 4.9 all-to-all-start
  527.0 4.6 all-to-all-done
  531.7 3.4 fusion.179
  540.3 4.5 collective-permute-start.1
  571.2 4.9 all-to-all-start
  578.9 4.6 all-to-all-done
  592.1 4.5 collective-permute-start.1
  623.0 4.9 all-to-all-start
  630.7 4.6 all-to-all-done
  643.9 4.5 collective-permute-start.1
  674.9 4.9 all-to-all-start
  682.5 4.6 all-to-all-done
  695.8 4.5 collective-permute-start.1
  726.7 4.9 all-to-all-start
  734.3 4.6 all-to-all-done
  (1284 shorter events, 465.4 us)
Async XLA Ops:
  5.3 14.8 %all-to-all-start.1 = ((s32[2,32,256]{2,0,1:T(2,128)}), s32[2,32,256]{2,0,1:T(2,128)S(1)}, u32[]{:S(2)}, u32[]{:S(2)}) async-start(s32[2,32,256]{2,0,1:T(2,128)} %copy.60), calls=%async_computation.1 | async-start | bytes 131072 | tf_op jit(solution)/shard_map/all_to_all | solution.py:174
  20.7 51.6 %collective-permute-start = (f32[1,16,128]{2,1,0:T(8,128)S(1)}, f32[1,16,128]{2,1,0:T(8,128)S(1)}, u32[]{:S(2)}, u32[]{:S(2)}) collective-permute-start(f32[1,16,128]{2,1,0:T(8,128)S(1)} %get-tuple-element.600), channel_id=1, source_target_pairs={{4,0},{8,4},{12,8},{16,12},{20,16},{24,20},{28,24},{5,1},{9,5},{13... | collective-permute-start | bytes 24584 | tf_op jit(solution)/shard_map/while/body/eval_jaxpr/ppermute | solution.py:15
  22.0 50.4 %collective-permute-start.1 = (f32[1,16,128]{2,1,0:T(8,128)S(1)}, f32[1,16,128]{2,1,0:T(8,128)S(1)}, u32[]{:S(2)}, u32[]{:S(2)}) collective-permute-start(f32[1,16,128]{2,1,0:T(8,128)S(1)} %get-tuple-element.603), channel_id=1, source_target_pairs={{0,4},{4,8},{8,12},{12,16},{16,20},{20,24},{24,28},{1,5},{5,9},{9,... | collective-permute-start | bytes 24584 | tf_op jit(solution)/shard_map/while/body/eval_jaxpr/ppermute | solution.py:15
  26.8 33.6 %collective-permute-start.3 = (f32[5,128]{1,0:T(8,128)S(1)}, f32[5,128]{1,0:T(8,128)S(1)}, u32[]{:S(2)}, u32[]{:S(2)}) collective-permute-start(f32[5,128]{1,0:T(8,128)S(1)} %pad_maximum_fusion.5), channel_id=1, source_target_pairs={{0,1},{1,2},{2,3},{4,5},{5,6},{6,7},{8,9},{9,10},{10,11},{12,13},{... | collective-permute-start | bytes 7688 | tf_op jit(solution)/shard_map/while/body/eval_jaxpr/ppermute | solution.py:15
  28.3 32.2 %collective-permute-start.2 = (f32[5,128]{1,0:T(8,128)S(1)}, f32[5,128]{1,0:T(8,128)S(1)}, u32[]{:S(2)}, u32[]{:S(2)}) collective-permute-start(f32[5,128]{1,0:T(8,128)S(1)} %pad_maximum_fusion.4), channel_id=1, source_target_pairs={{1,0},{2,1},{3,2},{5,4},{6,5},{7,6},{9,8},{10,9},{11,10},{13,12},{... | collective-permute-start | bytes 7688 | tf_op jit(solution)/shard_map/while/body/eval_jaxpr/ppermute | solution.py:15
  52.9 12.3 %all-to-all-start = ((f32[32,2,1,256]{3,2,1,0:T(1,128)}), f32[32,2,1,256]{3,2,1,0:T(1,128)S(1)}, u32[]{:S(2)}, u32[]{:S(2)}) async-start(f32[32,2,1,256]{3,2,1,0:T(1,128)} %constant_dynamic-update-slice_fusion.101), calls=%async_computation | async-start | bytes 131072 | tf_op jit(solution)/shard_map/while/body/eval_jaxpr/all_to_all | solution.py:113
  72.5 51.6 %collective-permute-start = (f32[1,16,128]{2,1,0:T(8,128)S(1)}, f32[1,16,128]{2,1,0:T(8,128)S(1)}, u32[]{:S(2)}, u32[]{:S(2)}) collective-permute-start(f32[1,16,128]{2,1,0:T(8,128)S(1)} %get-tuple-element.600), channel_id=1, source_target_pairs={{4,0},{8,4},{12,8},{16,12},{20,16},{24,20},{28,24},{5,1},{9,5},{13... | collective-permute-start | bytes 24584 | tf_op jit(solution)/shard_map/while/body/eval_jaxpr/ppermute | solution.py:15
  73.8 50.4 %collective-permute-start.1 = (f32[1,16,128]{2,1,0:T(8,128)S(1)}, f32[1,16,128]{2,1,0:T(8,128)S(1)}, u32[]{:S(2)}, u32[]{:S(2)}) collective-permute-start(f32[1,16,128]{2,1,0:T(8,128)S(1)} %get-tuple-element.603), channel_id=1, source_target_pairs={{0,4},{4,8},{8,12},{12,16},{16,20},{20,24},{24,28},{1,5},{5,9},{9,... | collective-permute-start | bytes 24584 | tf_op jit(solution)/shard_map/while/body/eval_jaxpr/ppermute | solution.py:15
  78.6 33.6 %collective-permute-start.3 = (f32[5,128]{1,0:T(8,128)S(1)}, f32[5,128]{1,0:T(8,128)S(1)}, u32[]{:S(2)}, u32[]{:S(2)}) collective-permute-start(f32[5,128]{1,0:T(8,128)S(1)} %pad_maximum_fusion.5), channel_id=1, source_target_pairs={{0,1},{1,2},{2,3},{4,5},{5,6},{6,7},{8,9},{9,10},{10,11},{12,13},{... | collective-permute-start | bytes 7688 | tf_op jit(solution)/shard_map/while/body/eval_jaxpr/ppermute | solution.py:15
  80.1 32.2 %collective-permute-start.2 = (f32[5,128]{1,0:T(8,128)S(1)}, f32[5,128]{1,0:T(8,128)S(1)}, u32[]{:S(2)}, u32[]{:S(2)}) collective-permute-start(f32[5,128]{1,0:T(8,128)S(1)} %pad_maximum_fusion.4), channel_id=1, source_target_pairs={{1,0},{2,1},{3,2},{5,4},{6,5},{7,6},{9,8},{10,9},{11,10},{13,12},{... | collective-permute-start | bytes 7688 | tf_op jit(solution)/shard_map/while/body/eval_jaxpr/ppermute | solution.py:15
  104.8 12.3 %all-to-all-start = ((f32[32,2,1,256]{3,2,1,0:T(1,128)}), f32[32,2,1,256]{3,2,1,0:T(1,128)S(1)}, u32[]{:S(2)}, u32[]{:S(2)}) async-start(f32[32,2,1,256]{3,2,1,0:T(1,128)} %constant_dynamic-update-slice_fusion.101), calls=%async_computation | async-start | bytes 131072 | tf_op jit(solution)/shard_map/while/body/eval_jaxpr/all_to_all | solution.py:113
  124.4 51.6 %collective-permute-start = (f32[1,16,128]{2,1,0:T(8,128)S(1)}, f32[1,16,128]{2,1,0:T(8,128)S(1)}, u32[]{:S(2)}, u32[]{:S(2)}) collective-permute-start(f32[1,16,128]{2,1,0:T(8,128)S(1)} %get-tuple-element.600), channel_id=1, source_target_pairs={{4,0},{8,4},{12,8},{16,12},{20,16},{24,20},{28,24},{5,1},{9,5},{13... | collective-permute-start | bytes 24584 | tf_op jit(solution)/shard_map/while/body/eval_jaxpr/ppermute | solution.py:15
  125.7 50.4 %collective-permute-start.1 = (f32[1,16,128]{2,1,0:T(8,128)S(1)}, f32[1,16,128]{2,1,0:T(8,128)S(1)}, u32[]{:S(2)}, u32[]{:S(2)}) collective-permute-start(f32[1,16,128]{2,1,0:T(8,128)S(1)} %get-tuple-element.603), channel_id=1, source_target_pairs={{0,4},{4,8},{8,12},{12,16},{16,20},{20,24},{24,28},{1,5},{5,9},{9,... | collective-permute-start | bytes 24584 | tf_op jit(solution)/shard_map/while/body/eval_jaxpr/ppermute | solution.py:15
  130.4 33.6 %collective-permute-start.3 = (f32[5,128]{1,0:T(8,128)S(1)}, f32[5,128]{1,0:T(8,128)S(1)}, u32[]{:S(2)}, u32[]{:S(2)}) collective-permute-start(f32[5,128]{1,0:T(8,128)S(1)} %pad_maximum_fusion.5), channel_id=1, source_target_pairs={{0,1},{1,2},{2,3},{4,5},{5,6},{6,7},{8,9},{9,10},{10,11},{12,13},{... | collective-permute-start | bytes 7688 | tf_op jit(solution)/shard_map/while/body/eval_jaxpr/ppermute | solution.py:15
  131.9 32.2 %collective-permute-start.2 = (f32[5,128]{1,0:T(8,128)S(1)}, f32[5,128]{1,0:T(8,128)S(1)}, u32[]{:S(2)}, u32[]{:S(2)}) collective-permute-start(f32[5,128]{1,0:T(8,128)S(1)} %pad_maximum_fusion.4), channel_id=1, source_target_pairs={{1,0},{2,1},{3,2},{5,4},{6,5},{7,6},{9,8},{10,9},{11,10},{13,12},{... | collective-permute-start | bytes 7688 | tf_op jit(solution)/shard_map/while/body/eval_jaxpr/ppermute | solution.py:15
  176.2 51.6 %collective-permute-start = (f32[1,16,128]{2,1,0:T(8,128)S(1)}, f32[1,16,128]{2,1,0:T(8,128)S(1)}, u32[]{:S(2)}, u32[]{:S(2)}) collective-permute-start(f32[1,16,128]{2,1,0:T(8,128)S(1)} %get-tuple-element.600), channel_id=1, source_target_pairs={{4,0},{8,4},{12,8},{16,12},{20,16},{24,20},{28,24},{5,1},{9,5},{13... | collective-permute-start | bytes 24584 | tf_op jit(solution)/shard_map/while/body/eval_jaxpr/ppermute | solution.py:15
  177.5 50.4 %collective-permute-start.1 = (f32[1,16,128]{2,1,0:T(8,128)S(1)}, f32[1,16,128]{2,1,0:T(8,128)S(1)}, u32[]{:S(2)}, u32[]{:S(2)}) collective-permute-start(f32[1,16,128]{2,1,0:T(8,128)S(1)} %get-tuple-element.603), channel_id=1, source_target_pairs={{0,4},{4,8},{8,12},{12,16},{16,20},{20,24},{24,28},{1,5},{5,9},{9,... | collective-permute-start | bytes 24584 | tf_op jit(solution)/shard_map/while/body/eval_jaxpr/ppermute | solution.py:15
  182.3 33.6 %collective-permute-start.3 = (f32[5,128]{1,0:T(8,128)S(1)}, f32[5,128]{1,0:T(8,128)S(1)}, u32[]{:S(2)}, u32[]{:S(2)}) collective-permute-start(f32[5,128]{1,0:T(8,128)S(1)} %pad_maximum_fusion.5), channel_id=1, source_target_pairs={{0,1},{1,2},{2,3},{4,5},{5,6},{6,7},{8,9},{9,10},{10,11},{12,13},{... | collective-permute-start | bytes 7688 | tf_op jit(solution)/shard_map/while/body/eval_jaxpr/ppermute | solution.py:15
  183.8 32.2 %collective-permute-start.2 = (f32[5,128]{1,0:T(8,128)S(1)}, f32[5,128]{1,0:T(8,128)S(1)}, u32[]{:S(2)}, u32[]{:S(2)}) collective-permute-start(f32[5,128]{1,0:T(8,128)S(1)} %pad_maximum_fusion.4), channel_id=1, source_target_pairs={{1,0},{2,1},{3,2},{5,4},{6,5},{7,6},{9,8},{10,9},{11,10},{13,12},{... | collective-permute-start | bytes 7688 | tf_op jit(solution)/shard_map/while/body/eval_jaxpr/ppermute | solution.py:15
  228.0 51.6 %collective-permute-start = (f32[1,16,128]{2,1,0:T(8,128)S(1)}, f32[1,16,128]{2,1,0:T(8,128)S(1)}, u32[]{:S(2)}, u32[]{:S(2)}) collective-permute-start(f32[1,16,128]{2,1,0:T(8,128)S(1)} %get-tuple-element.600), channel_id=1, source_target_pairs={{4,0},{8,4},{12,8},{16,12},{20,16},{24,20},{28,24},{5,1},{9,5},{13... | collective-permute-start | bytes 24584 | tf_op jit(solution)/shard_map/while/body/eval_jaxpr/ppermute | solution.py:15
  229.3 50.4 %collective-permute-start.1 = (f32[1,16,128]{2,1,0:T(8,128)S(1)}, f32[1,16,128]{2,1,0:T(8,128)S(1)}, u32[]{:S(2)}, u32[]{:S(2)}) collective-permute-start(f32[1,16,128]{2,1,0:T(8,128)S(1)} %get-tuple-element.603), channel_id=1, source_target_pairs={{0,4},{4,8},{8,12},{12,16},{16,20},{20,24},{24,28},{1,5},{5,9},{9,... | collective-permute-start | bytes 24584 | tf_op jit(solution)/shard_map/while/body/eval_jaxpr/ppermute | solution.py:15
  234.1 33.6 %collective-permute-start.3 = (f32[5,128]{1,0:T(8,128)S(1)}, f32[5,128]{1,0:T(8,128)S(1)}, u32[]{:S(2)}, u32[]{:S(2)}) collective-permute-start(f32[5,128]{1,0:T(8,128)S(1)} %pad_maximum_fusion.5), channel_id=1, source_target_pairs={{0,1},{1,2},{2,3},{4,5},{5,6},{6,7},{8,9},{9,10},{10,11},{12,13},{... | collective-permute-start | bytes 7688 | tf_op jit(solution)/shard_map/while/body/eval_jaxpr/ppermute | solution.py:15
  235.6 32.2 %collective-permute-start.2 = (f32[5,128]{1,0:T(8,128)S(1)}, f32[5,128]{1,0:T(8,128)S(1)}, u32[]{:S(2)}, u32[]{:S(2)}) collective-permute-start(f32[5,128]{1,0:T(8,128)S(1)} %pad_maximum_fusion.4), channel_id=1, source_target_pairs={{1,0},{2,1},{3,2},{5,4},{6,5},{7,6},{9,8},{10,9},{11,10},{13,12},{... | collective-permute-start | bytes 7688 | tf_op jit(solution)/shard_map/while/body/eval_jaxpr/ppermute | solution.py:15
  260.3 12.3 %all-to-all-start = ((f32[32,2,1,256]{3,2,1,0:T(1,128)}), f32[32,2,1,256]{3,2,1,0:T(1,128)S(1)}, u32[]{:S(2)}, u32[]{:S(2)}) async-start(f32[32,2,1,256]{3,2,1,0:T(1,128)} %constant_dynamic-update-slice_fusion.101), calls=%async_computation | async-start | bytes 131072 | tf_op jit(solution)/shard_map/while/body/eval_jaxpr/all_to_all | solution.py:113
  279.8 51.6 %collective-permute-start = (f32[1,16,128]{2,1,0:T(8,128)S(1)}, f32[1,16,128]{2,1,0:T(8,128)S(1)}, u32[]{:S(2)}, u32[]{:S(2)}) collective-permute-start(f32[1,16,128]{2,1,0:T(8,128)S(1)} %get-tuple-element.600), channel_id=1, source_target_pairs={{4,0},{8,4},{12,8},{16,12},{20,16},{24,20},{28,24},{5,1},{9,5},{13... | collective-permute-start | bytes 24584 | tf_op jit(solution)/shard_map/while/body/eval_jaxpr/ppermute | solution.py:15
  281.1 50.4 %collective-permute-start.1 = (f32[1,16,128]{2,1,0:T(8,128)S(1)}, f32[1,16,128]{2,1,0:T(8,128)S(1)}, u32[]{:S(2)}, u32[]{:S(2)}) collective-permute-start(f32[1,16,128]{2,1,0:T(8,128)S(1)} %get-tuple-element.603), channel_id=1, source_target_pairs={{0,4},{4,8},{8,12},{12,16},{16,20},{20,24},{24,28},{1,5},{5,9},{9,... | collective-permute-start | bytes 24584 | tf_op jit(solution)/shard_map/while/body/eval_jaxpr/ppermute | solution.py:15
  285.9 33.6 %collective-permute-start.3 = (f32[5,128]{1,0:T(8,128)S(1)}, f32[5,128]{1,0:T(8,128)S(1)}, u32[]{:S(2)}, u32[]{:S(2)}) collective-permute-start(f32[5,128]{1,0:T(8,128)S(1)} %pad_maximum_fusion.5), channel_id=1, source_target_pairs={{0,1},{1,2},{2,3},{4,5},{5,6},{6,7},{8,9},{9,10},{10,11},{12,13},{... | collective-permute-start | bytes 7688 | tf_op jit(solution)/shard_map/while/body/eval_jaxpr/ppermute | solution.py:15
  287.4 32.2 %collective-permute-start.2 = (f32[5,128]{1,0:T(8,128)S(1)}, f32[5,128]{1,0:T(8,128)S(1)}, u32[]{:S(2)}, u32[]{:S(2)}) collective-permute-start(f32[5,128]{1,0:T(8,128)S(1)} %pad_maximum_fusion.4), channel_id=1, source_target_pairs={{1,0},{2,1},{3,2},{5,4},{6,5},{7,6},{9,8},{10,9},{11,10},{13,12},{... | collective-permute-start | bytes 7688 | tf_op jit(solution)/shard_map/while/body/eval_jaxpr/ppermute | solution.py:15
  331.7 51.6 %collective-permute-start = (f32[1,16,128]{2,1,0:T(8,128)S(1)}, f32[1,16,128]{2,1,0:T(8,128)S(1)}, u32[]{:S(2)}, u32[]{:S(2)}) collective-permute-start(f32[1,16,128]{2,1,0:T(8,128)S(1)} %get-tuple-element.600), channel_id=1, source_target_pairs={{4,0},{8,4},{12,8},{16,12},{20,16},{24,20},{28,24},{5,1},{9,5},{13... | collective-permute-start | bytes 24584 | tf_op jit(solution)/shard_map/while/body/eval_jaxpr/ppermute | solution.py:15
  333.0 50.4 %collective-permute-start.1 = (f32[1,16,128]{2,1,0:T(8,128)S(1)}, f32[1,16,128]{2,1,0:T(8,128)S(1)}, u32[]{:S(2)}, u32[]{:S(2)}) collective-permute-start(f32[1,16,128]{2,1,0:T(8,128)S(1)} %get-tuple-element.603), channel_id=1, source_target_pairs={{0,4},{4,8},{8,12},{12,16},{16,20},{20,24},{24,28},{1,5},{5,9},{9,... | collective-permute-start | bytes 24584 | tf_op jit(solution)/shard_map/while/body/eval_jaxpr/ppermute | solution.py:15
  337.8 33.6 %collective-permute-start.3 = (f32[5,128]{1,0:T(8,128)S(1)}, f32[5,128]{1,0:T(8,128)S(1)}, u32[]{:S(2)}, u32[]{:S(2)}) collective-permute-start(f32[5,128]{1,0:T(8,128)S(1)} %pad_maximum_fusion.5), channel_id=1, source_target_pairs={{0,1},{1,2},{2,3},{4,5},{5,6},{6,7},{8,9},{9,10},{10,11},{12,13},{... | collective-permute-start | bytes 7688 | tf_op jit(solution)/shard_map/while/body/eval_jaxpr/ppermute | solution.py:15
  339.2 32.2 %collective-permute-start.2 = (f32[5,128]{1,0:T(8,128)S(1)}, f32[5,128]{1,0:T(8,128)S(1)}, u32[]{:S(2)}, u32[]{:S(2)}) collective-permute-start(f32[5,128]{1,0:T(8,128)S(1)} %pad_maximum_fusion.4), channel_id=1, source_target_pairs={{1,0},{2,1},{3,2},{5,4},{6,5},{7,6},{9,8},{10,9},{11,10},{13,12},{... | collective-permute-start | bytes 7688 | tf_op jit(solution)/shard_map/while/body/eval_jaxpr/ppermute | solution.py:15
  363.9 12.3 %all-to-all-start = ((f32[32,2,1,256]{3,2,1,0:T(1,128)}), f32[32,2,1,256]{3,2,1,0:T(1,128)S(1)}, u32[]{:S(2)}, u32[]{:S(2)}) async-start(f32[32,2,1,256]{3,2,1,0:T(1,128)} %constant_dynamic-update-slice_fusion.101), calls=%async_computation | async-start | bytes 131072 | tf_op jit(solution)/shard_map/while/body/eval_jaxpr/all_to_all | solution.py:113
  383.5 51.6 %collective-permute-start = (f32[1,16,128]{2,1,0:T(8,128)S(1)}, f32[1,16,128]{2,1,0:T(8,128)S(1)}, u32[]{:S(2)}, u32[]{:S(2)}) collective-permute-start(f32[1,16,128]{2,1,0:T(8,128)S(1)} %get-tuple-element.600), channel_id=1, source_target_pairs={{4,0},{8,4},{12,8},{16,12},{20,16},{24,20},{28,24},{5,1},{9,5},{13... | collective-permute-start | bytes 24584 | tf_op jit(solution)/shard_map/while/body/eval_jaxpr/ppermute | solution.py:15
  384.8 50.4 %collective-permute-start.1 = (f32[1,16,128]{2,1,0:T(8,128)S(1)}, f32[1,16,128]{2,1,0:T(8,128)S(1)}, u32[]{:S(2)}, u32[]{:S(2)}) collective-permute-start(f32[1,16,128]{2,1,0:T(8,128)S(1)} %get-tuple-element.603), channel_id=1, source_target_pairs={{0,4},{4,8},{8,12},{12,16},{16,20},{20,24},{24,28},{1,5},{5,9},{9,... | collective-permute-start | bytes 24584 | tf_op jit(solution)/shard_map/while/body/eval_jaxpr/ppermute | solution.py:15
  389.6 33.6 %collective-permute-start.3 = (f32[5,128]{1,0:T(8,128)S(1)}, f32[5,128]{1,0:T(8,128)S(1)}, u32[]{:S(2)}, u32[]{:S(2)}) collective-permute-start(f32[5,128]{1,0:T(8,128)S(1)} %pad_maximum_fusion.5), channel_id=1, source_target_pairs={{0,1},{1,2},{2,3},{4,5},{5,6},{6,7},{8,9},{9,10},{10,11},{12,13},{... | collective-permute-start | bytes 7688 | tf_op jit(solution)/shard_map/while/body/eval_jaxpr/ppermute | solution.py:15
  391.1 32.2 %collective-permute-start.2 = (f32[5,128]{1,0:T(8,128)S(1)}, f32[5,128]{1,0:T(8,128)S(1)}, u32[]{:S(2)}, u32[]{:S(2)}) collective-permute-start(f32[5,128]{1,0:T(8,128)S(1)} %pad_maximum_fusion.4), channel_id=1, source_target_pairs={{1,0},{2,1},{3,2},{5,4},{6,5},{7,6},{9,8},{10,9},{11,10},{13,12},{... | collective-permute-start | bytes 7688 | tf_op jit(solution)/shard_map/while/body/eval_jaxpr/ppermute | solution.py:15
  435.3 51.6 %collective-permute-start = (f32[1,16,128]{2,1,0:T(8,128)S(1)}, f32[1,16,128]{2,1,0:T(8,128)S(1)}, u32[]{:S(2)}, u32[]{:S(2)}) collective-permute-start(f32[1,16,128]{2,1,0:T(8,128)S(1)} %get-tuple-element.600), channel_id=1, source_target_pairs={{4,0},{8,4},{12,8},{16,12},{20,16},{24,20},{28,24},{5,1},{9,5},{13... | collective-permute-start | bytes 24584 | tf_op jit(solution)/shard_map/while/body/eval_jaxpr/ppermute | solution.py:15
  436.6 50.4 %collective-permute-start.1 = (f32[1,16,128]{2,1,0:T(8,128)S(1)}, f32[1,16,128]{2,1,0:T(8,128)S(1)}, u32[]{:S(2)}, u32[]{:S(2)}) collective-permute-start(f32[1,16,128]{2,1,0:T(8,128)S(1)} %get-tuple-element.603), channel_id=1, source_target_pairs={{0,4},{4,8},{8,12},{12,16},{16,20},{20,24},{24,28},{1,5},{5,9},{9,... | collective-permute-start | bytes 24584 | tf_op jit(solution)/shard_map/while/body/eval_jaxpr/ppermute | solution.py:15
  441.4 33.6 %collective-permute-start.3 = (f32[5,128]{1,0:T(8,128)S(1)}, f32[5,128]{1,0:T(8,128)S(1)}, u32[]{:S(2)}, u32[]{:S(2)}) collective-permute-start(f32[5,128]{1,0:T(8,128)S(1)} %pad_maximum_fusion.5), channel_id=1, source_target_pairs={{0,1},{1,2},{2,3},{4,5},{5,6},{6,7},{8,9},{9,10},{10,11},{12,13},{... | collective-permute-start | bytes 7688 | tf_op jit(solution)/shard_map/while/body/eval_jaxpr/ppermute | solution.py:15
  442.9 32.2 %collective-permute-start.2 = (f32[5,128]{1,0:T(8,128)S(1)}, f32[5,128]{1,0:T(8,128)S(1)}, u32[]{:S(2)}, u32[]{:S(2)}) collective-permute-start(f32[5,128]{1,0:T(8,128)S(1)} %pad_maximum_fusion.4), channel_id=1, source_target_pairs={{1,0},{2,1},{3,2},{5,4},{6,5},{7,6},{9,8},{10,9},{11,10},{13,12},{... | collective-permute-start | bytes 7688 | tf_op jit(solution)/shard_map/while/body/eval_jaxpr/ppermute | solution.py:15
  487.1 51.6 %collective-permute-start = (f32[1,16,128]{2,1,0:T(8,128)S(1)}, f32[1,16,128]{2,1,0:T(8,128)S(1)}, u32[]{:S(2)}, u32[]{:S(2)}) collective-permute-start(f32[1,16,128]{2,1,0:T(8,128)S(1)} %get-tuple-element.600), channel_id=1, source_target_pairs={{4,0},{8,4},{12,8},{16,12},{20,16},{24,20},{28,24},{5,1},{9,5},{13... | collective-permute-start | bytes 24584 | tf_op jit(solution)/shard_map/while/body/eval_jaxpr/ppermute | solution.py:15
  488.4 50.4 %collective-permute-start.1 = (f32[1,16,128]{2,1,0:T(8,128)S(1)}, f32[1,16,128]{2,1,0:T(8,128)S(1)}, u32[]{:S(2)}, u32[]{:S(2)}) collective-permute-start(f32[1,16,128]{2,1,0:T(8,128)S(1)} %get-tuple-element.603), channel_id=1, source_target_pairs={{0,4},{4,8},{8,12},{12,16},{16,20},{20,24},{24,28},{1,5},{5,9},{9,... | collective-permute-start | bytes 24584 | tf_op jit(solution)/shard_map/while/body/eval_jaxpr/ppermute | solution.py:15
  493.2 33.6 %collective-permute-start.3 = (f32[5,128]{1,0:T(8,128)S(1)}, f32[5,128]{1,0:T(8,128)S(1)}, u32[]{:S(2)}, u32[]{:S(2)}) collective-permute-start(f32[5,128]{1,0:T(8,128)S(1)} %pad_maximum_fusion.5), channel_id=1, source_target_pairs={{0,1},{1,2},{2,3},{4,5},{5,6},{6,7},{8,9},{9,10},{10,11},{12,13},{... | collective-permute-start | bytes 7688 | tf_op jit(solution)/shard_map/while/body/eval_jaxpr/ppermute | solution.py:15
  494.7 32.2 %collective-permute-start.2 = (f32[5,128]{1,0:T(8,128)S(1)}, f32[5,128]{1,0:T(8,128)S(1)}, u32[]{:S(2)}, u32[]{:S(2)}) collective-permute-start(f32[5,128]{1,0:T(8,128)S(1)} %pad_maximum_fusion.4), channel_id=1, source_target_pairs={{1,0},{2,1},{3,2},{5,4},{6,5},{7,6},{9,8},{10,9},{11,10},{13,12},{... | collective-permute-start | bytes 7688 | tf_op jit(solution)/shard_map/while/body/eval_jaxpr/ppermute | solution.py:15
  519.4 12.3 %all-to-all-start = ((f32[32,2,1,256]{3,2,1,0:T(1,128)}), f32[32,2,1,256]{3,2,1,0:T(1,128)S(1)}, u32[]{:S(2)}, u32[]{:S(2)}) async-start(f32[32,2,1,256]{3,2,1,0:T(1,128)} %constant_dynamic-update-slice_fusion.101), calls=%async_computation | async-start | bytes 131072 | tf_op jit(solution)/shard_map/while/body/eval_jaxpr/all_to_all | solution.py:113
  539.0 51.6 %collective-permute-start = (f32[1,16,128]{2,1,0:T(8,128)S(1)}, f32[1,16,128]{2,1,0:T(8,128)S(1)}, u32[]{:S(2)}, u32[]{:S(2)}) collective-permute-start(f32[1,16,128]{2,1,0:T(8,128)S(1)} %get-tuple-element.600), channel_id=1, source_target_pairs={{4,0},{8,4},{12,8},{16,12},{20,16},{24,20},{28,24},{5,1},{9,5},{13... | collective-permute-start | bytes 24584 | tf_op jit(solution)/shard_map/while/body/eval_jaxpr/ppermute | solution.py:15
  540.3 50.4 %collective-permute-start.1 = (f32[1,16,128]{2,1,0:T(8,128)S(1)}, f32[1,16,128]{2,1,0:T(8,128)S(1)}, u32[]{:S(2)}, u32[]{:S(2)}) collective-permute-start(f32[1,16,128]{2,1,0:T(8,128)S(1)} %get-tuple-element.603), channel_id=1, source_target_pairs={{0,4},{4,8},{8,12},{12,16},{16,20},{20,24},{24,28},{1,5},{5,9},{9,... | collective-permute-start | bytes 24584 | tf_op jit(solution)/shard_map/while/body/eval_jaxpr/ppermute | solution.py:15
  545.1 33.6 %collective-permute-start.3 = (f32[5,128]{1,0:T(8,128)S(1)}, f32[5,128]{1,0:T(8,128)S(1)}, u32[]{:S(2)}, u32[]{:S(2)}) collective-permute-start(f32[5,128]{1,0:T(8,128)S(1)} %pad_maximum_fusion.5), channel_id=1, source_target_pairs={{0,1},{1,2},{2,3},{4,5},{5,6},{6,7},{8,9},{9,10},{10,11},{12,13},{... | collective-permute-start | bytes 7688 | tf_op jit(solution)/shard_map/while/body/eval_jaxpr/ppermute | solution.py:15
  546.6 32.2 %collective-permute-start.2 = (f32[5,128]{1,0:T(8,128)S(1)}, f32[5,128]{1,0:T(8,128)S(1)}, u32[]{:S(2)}, u32[]{:S(2)}) collective-permute-start(f32[5,128]{1,0:T(8,128)S(1)} %pad_maximum_fusion.4), channel_id=1, source_target_pairs={{1,0},{2,1},{3,2},{5,4},{6,5},{7,6},{9,8},{10,9},{11,10},{13,12},{... | collective-permute-start | bytes 7688 | tf_op jit(solution)/shard_map/while/body/eval_jaxpr/ppermute | solution.py:15
  590.8 51.6 %collective-permute-start = (f32[1,16,128]{2,1,0:T(8,128)S(1)}, f32[1,16,128]{2,1,0:T(8,128)S(1)}, u32[]{:S(2)}, u32[]{:S(2)}) collective-permute-start(f32[1,16,128]{2,1,0:T(8,128)S(1)} %get-tuple-element.600), channel_id=1, source_target_pairs={{4,0},{8,4},{12,8},{16,12},{20,16},{24,20},{28,24},{5,1},{9,5},{13... | collective-permute-start | bytes 24584 | tf_op jit(solution)/shard_map/while/body/eval_jaxpr/ppermute | solution.py:15
  592.1 50.4 %collective-permute-start.1 = (f32[1,16,128]{2,1,0:T(8,128)S(1)}, f32[1,16,128]{2,1,0:T(8,128)S(1)}, u32[]{:S(2)}, u32[]{:S(2)}) collective-permute-start(f32[1,16,128]{2,1,0:T(8,128)S(1)} %get-tuple-element.603), channel_id=1, source_target_pairs={{0,4},{4,8},{8,12},{12,16},{16,20},{20,24},{24,28},{1,5},{5,9},{9,... | collective-permute-start | bytes 24584 | tf_op jit(solution)/shard_map/while/body/eval_jaxpr/ppermute | solution.py:15
  596.9 33.6 %collective-permute-start.3 = (f32[5,128]{1,0:T(8,128)S(1)}, f32[5,128]{1,0:T(8,128)S(1)}, u32[]{:S(2)}, u32[]{:S(2)}) collective-permute-start(f32[5,128]{1,0:T(8,128)S(1)} %pad_maximum_fusion.5), channel_id=1, source_target_pairs={{0,1},{1,2},{2,3},{4,5},{5,6},{6,7},{8,9},{9,10},{10,11},{12,13},{... | collective-permute-start | bytes 7688 | tf_op jit(solution)/shard_map/while/body/eval_jaxpr/ppermute | solution.py:15
  598.4 32.2 %collective-permute-start.2 = (f32[5,128]{1,0:T(8,128)S(1)}, f32[5,128]{1,0:T(8,128)S(1)}, u32[]{:S(2)}, u32[]{:S(2)}) collective-permute-start(f32[5,128]{1,0:T(8,128)S(1)} %pad_maximum_fusion.4), channel_id=1, source_target_pairs={{1,0},{2,1},{3,2},{5,4},{6,5},{7,6},{9,8},{10,9},{11,10},{13,12},{... | collective-permute-start | bytes 7688 | tf_op jit(solution)/shard_map/while/body/eval_jaxpr/ppermute | solution.py:15
  623.0 12.3 %all-to-all-start = ((f32[32,2,1,256]{3,2,1,0:T(1,128)}), f32[32,2,1,256]{3,2,1,0:T(1,128)S(1)}, u32[]{:S(2)}, u32[]{:S(2)}) async-start(f32[32,2,1,256]{3,2,1,0:T(1,128)} %constant_dynamic-update-slice_fusion.101), calls=%async_computation | async-start | bytes 131072 | tf_op jit(solution)/shard_map/while/body/eval_jaxpr/all_to_all | solution.py:113
  642.6 51.6 %collective-permute-start = (f32[1,16,128]{2,1,0:T(8,128)S(1)}, f32[1,16,128]{2,1,0:T(8,128)S(1)}, u32[]{:S(2)}, u32[]{:S(2)}) collective-permute-start(f32[1,16,128]{2,1,0:T(8,128)S(1)} %get-tuple-element.600), channel_id=1, source_target_pairs={{4,0},{8,4},{12,8},{16,12},{20,16},{24,20},{28,24},{5,1},{9,5},{13... | collective-permute-start | bytes 24584 | tf_op jit(solution)/shard_map/while/body/eval_jaxpr/ppermute | solution.py:15
  643.9 50.4 %collective-permute-start.1 = (f32[1,16,128]{2,1,0:T(8,128)S(1)}, f32[1,16,128]{2,1,0:T(8,128)S(1)}, u32[]{:S(2)}, u32[]{:S(2)}) collective-permute-start(f32[1,16,128]{2,1,0:T(8,128)S(1)} %get-tuple-element.603), channel_id=1, source_target_pairs={{0,4},{4,8},{8,12},{12,16},{16,20},{20,24},{24,28},{1,5},{5,9},{9,... | collective-permute-start | bytes 24584 | tf_op jit(solution)/shard_map/while/body/eval_jaxpr/ppermute | solution.py:15
  648.7 33.6 %collective-permute-start.3 = (f32[5,128]{1,0:T(8,128)S(1)}, f32[5,128]{1,0:T(8,128)S(1)}, u32[]{:S(2)}, u32[]{:S(2)}) collective-permute-start(f32[5,128]{1,0:T(8,128)S(1)} %pad_maximum_fusion.5), channel_id=1, source_target_pairs={{0,1},{1,2},{2,3},{4,5},{5,6},{6,7},{8,9},{9,10},{10,11},{12,13},{... | collective-permute-start | bytes 7688 | tf_op jit(solution)/shard_map/while/body/eval_jaxpr/ppermute | solution.py:15
  650.2 32.2 %collective-permute-start.2 = (f32[5,128]{1,0:T(8,128)S(1)}, f32[5,128]{1,0:T(8,128)S(1)}, u32[]{:S(2)}, u32[]{:S(2)}) collective-permute-start(f32[5,128]{1,0:T(8,128)S(1)} %pad_maximum_fusion.4), channel_id=1, source_target_pairs={{1,0},{2,1},{3,2},{5,4},{6,5},{7,6},{9,8},{10,9},{11,10},{13,12},{... | collective-permute-start | bytes 7688 | tf_op jit(solution)/shard_map/while/body/eval_jaxpr/ppermute | solution.py:15
  694.5 51.6 %collective-permute-start = (f32[1,16,128]{2,1,0:T(8,128)S(1)}, f32[1,16,128]{2,1,0:T(8,128)S(1)}, u32[]{:S(2)}, u32[]{:S(2)}) collective-permute-start(f32[1,16,128]{2,1,0:T(8,128)S(1)} %get-tuple-element.600), channel_id=1, source_target_pairs={{4,0},{8,4},{12,8},{16,12},{20,16},{24,20},{28,24},{5,1},{9,5},{13... | collective-permute-start | bytes 24584 | tf_op jit(solution)/shard_map/while/body/eval_jaxpr/ppermute | solution.py:15
  695.8 50.4 %collective-permute-start.1 = (f32[1,16,128]{2,1,0:T(8,128)S(1)}, f32[1,16,128]{2,1,0:T(8,128)S(1)}, u32[]{:S(2)}, u32[]{:S(2)}) collective-permute-start(f32[1,16,128]{2,1,0:T(8,128)S(1)} %get-tuple-element.603), channel_id=1, source_target_pairs={{0,4},{4,8},{8,12},{12,16},{16,20},{20,24},{24,28},{1,5},{5,9},{9,... | collective-permute-start | bytes 24584 | tf_op jit(solution)/shard_map/while/body/eval_jaxpr/ppermute | solution.py:15
  700.5 33.6 %collective-permute-start.3 = (f32[5,128]{1,0:T(8,128)S(1)}, f32[5,128]{1,0:T(8,128)S(1)}, u32[]{:S(2)}, u32[]{:S(2)}) collective-permute-start(f32[5,128]{1,0:T(8,128)S(1)} %pad_maximum_fusion.5), channel_id=1, source_target_pairs={{0,1},{1,2},{2,3},{4,5},{5,6},{6,7},{8,9},{9,10},{10,11},{12,13},{... | collective-permute-start | bytes 7688 | tf_op jit(solution)/shard_map/while/body/eval_jaxpr/ppermute | solution.py:15
  702.0 32.2 %collective-permute-start.2 = (f32[5,128]{1,0:T(8,128)S(1)}, f32[5,128]{1,0:T(8,128)S(1)}, u32[]{:S(2)}, u32[]{:S(2)}) collective-permute-start(f32[5,128]{1,0:T(8,128)S(1)} %pad_maximum_fusion.4), channel_id=1, source_target_pairs={{1,0},{2,1},{3,2},{5,4},{6,5},{7,6},{9,8},{10,9},{11,10},{13,12},{... | collective-permute-start | bytes 7688 | tf_op jit(solution)/shard_map/while/body/eval_jaxpr/ppermute | solution.py:15
  726.7 12.3 %all-to-all-start = ((f32[32,2,1,256]{3,2,1,0:T(1,128)}), f32[32,2,1,256]{3,2,1,0:T(1,128)S(1)}, u32[]{:S(2)}, u32[]{:S(2)}) async-start(f32[32,2,1,256]{3,2,1,0:T(1,128)} %constant_dynamic-update-slice_fusion.101), calls=%async_computation | async-start | bytes 131072 | tf_op jit(solution)/shard_map/while/body/eval_jaxpr/all_to_all | solution.py:113
  (81 other events, 514.8 us)
